TPU v7x, 32 devices: a whole 2x2x4 slice. The times are simulated.
32 devices in a mesh: dp: 2 (over x), col: 4 (over z), row: 4 (over y, core).
Axes of the slice: x: 2, y: 2, z: 4, core: 2. Of those that a mesh axis runs over, the one named last changes fastest.
Arguments:
- hidden: bfloat16 [256, 1024], P('dp', 'row'), parts along dimension 0
- cache_len: int32 [256], P('dp'), parts along dimension 0
- k_cache: bfloat16 [2, 256, 16, 512, 64], P(None, 'dp', ('col', 'row')), parts along dimension 1
- v_cache: bfloat16 [2, 256, 16, 512, 64], P(None, 'dp', ('col', 'row')), parts along dimension 1
- ln1_g: bfloat16 [2, 1024], P(None, 'row')
- ln1_b: bfloat16 [2, 1024], P(None, 'row')
- w_q: bfloat16 [2, 1024, 1024], P(None, 'row', 'col')
- b_q: bfloat16 [2, 1024], P(None, 'col')
- w_k: bfloat16 [2, 1024, 1024], P(None, 'row', 'col')
- b_k: bfloat16 [2, 1024], P(None, 'col')
- w_v: bfloat16 [2, 1024, 1024], P(None, 'row', 'col')
- b_v: bfloat16 [2, 1024], P(None, 'col')
- w_o: bfloat16 [2, 1024, 1024], P(None, 'col', 'row')
- b_o: bfloat16 [2, 1024], P(None, 'row')
- ln2_g: bfloat16 [2, 1024], P(None, 'row')
- ln2_b: bfloat16 [2, 1024], P(None, 'row')
- w_fc1: bfloat16 [2, 1024, 4096], P(None, 'row', 'col')
- b_fc1: bfloat16 [2, 4096], P(None, 'col')
- w_fc2: bfloat16 [2, 4096, 1024], P(None, 'col', 'row')
- b_fc2: bfloat16 [2, 1024], P(None, 'row')
Outputs:
- output 1: bfloat16 [256, 1024], P('dp', 'row'), parts along dimension 0
- output 2: bfloat16 [2, 256, 16, 64], P(None, 'dp', ('col', 'row')), parts along dimension 1
- output 3: bfloat16 [2, 256, 16, 64], P(None, 'dp', ('col', 'row')), parts along dimension 1
There are 2 independent parts. A program takes and returns all parts, laid end to end along the dimension named above; an argument that names none is the same for every part.
All inputs are finite; a program needn't handle non-finite values.
Results may differ from a plain program's by a relative error of at most 0.0190479.
Values are sent between devices in bfloat16 or wider.
A program may use at most 1 GiB of HBM per device.

v0:
```python
import jax
import jax.numpy as jnp
from jax import lax
from jax.sharding import PartitionSpec as P

EPS_LN = 1e-5


def attention(q_heads, k_fresh, v_fresh, k_layer, v_layer, lengths):
    scores = jnp.einsum("bhd,bhsd->bhs", q_heads, k_layer, preferred_element_type=jnp.float32)
    positions = jnp.arange(k_layer.shape[2])
    scores = jnp.where(positions[None, None, :] < lengths[:, None, None], scores, -jnp.inf)
    score_new = jnp.einsum("bhd,bhd->bh", q_heads, k_fresh, preferred_element_type=jnp.float32)
    peak = jnp.maximum(jnp.max(scores, axis=-1), score_new)
    exp_cache = jnp.exp(scores - peak[:, :, None])
    exp_new = jnp.exp(score_new - peak)
    total_mass = jnp.sum(exp_cache, axis=-1) + exp_new
    prob_cache = (exp_cache / total_mass[:, :, None]).astype(jnp.bfloat16)
    prob_new = (exp_new / total_mass).astype(jnp.bfloat16)
    mixed = jnp.einsum("bhs,bhsd->bhd", prob_cache, v_layer, preferred_element_type=jnp.float32)
    mixed = mixed + prob_new.astype(jnp.float32)[:, :, None] * v_fresh.astype(jnp.float32)
    return mixed.astype(jnp.bfloat16)


def solution(mesh):
    n_row = mesh.shape["row"]
    act_spec = P("dp", "row")
    cache_spec = P(None, "dp", ("col", "row"), None, None)
    fresh_spec = P(None, "dp", ("col", "row"), None)
    in_weight = P(None, "row", "col")
    out_weight = P(None, "col", "row")
    col_vec = P(None, "col")
    row_vec = P(None, "row")
    in_specs = (act_spec, P("dp"), cache_spec, cache_spec, row_vec, row_vec,
                in_weight, col_vec, in_weight, col_vec, in_weight, col_vec,
                out_weight, row_vec, row_vec, row_vec, in_weight, col_vec, out_weight, row_vec)

    def layer_norm(state, gain, shift):
        state_f32 = state.astype(jnp.float32)
        stats = jnp.stack([jnp.sum(state_f32, axis=-1), jnp.sum(state_f32 * state_f32, axis=-1)], axis=-1)
        stats = lax.psum(stats, "row")
        width = state.shape[-1] * n_row
        mean_val = stats[:, 0:1] / width
        variance = stats[:, 1:2] / width - mean_val * mean_val
        normed = (state_f32 - mean_val) * lax.rsqrt(variance + EPS_LN) * gain.astype(jnp.float32) + shift.astype(jnp.float32)
        return normed.astype(jnp.bfloat16)

    def head_projection(normed, weight, bias, scale):
        partial = jnp.dot(normed, weight, preferred_element_type=jnp.float32).astype(jnp.bfloat16)
        summed = lax.psum_scatter(partial, "row", scatter_dimension=1, tiled=True)
        width = summed.shape[1]
        bias_own = lax.dynamic_slice_in_dim(bias, lax.axis_index("row") * width, width)
        return ((summed.astype(jnp.float32) + bias_own.astype(jnp.float32)) * scale).astype(jnp.bfloat16)

    def local_step(hidden, cache_len, k_cache, v_cache, ln1_g, ln1_b, w_q, b_q, w_k, b_k, w_v, b_v,
                   w_o, b_o, ln2_g, ln2_b, w_fc1, b_fc1, w_fc2, b_fc2):
        batch_rows = hidden.shape[0]
        heads_dev = k_cache.shape[2]
        head_dim = k_cache.shape[4]
        scale = head_dim ** -0.5
        state = hidden
        k_rows = []
        v_rows = []
        for layer in range(w_q.shape[0]):
            normed = layer_norm(state, ln1_g[layer], ln1_b[layer])
            q_heads = head_projection(normed, w_q[layer], b_q[layer], scale).reshape(batch_rows, heads_dev, head_dim)
            k_fresh = head_projection(normed, w_k[layer], b_k[layer], 1.0).reshape(batch_rows, heads_dev, head_dim)
            v_fresh = head_projection(normed, w_v[layer], b_v[layer], 1.0).reshape(batch_rows, heads_dev, head_dim)
            attended = attention(q_heads, k_fresh, v_fresh, k_cache[layer], v_cache[layer], cache_len)
            gathered = lax.all_gather(attended.reshape(batch_rows, heads_dev * head_dim), "row", axis=1, tiled=True)
            proj_part = jnp.dot(gathered, w_o[layer], preferred_element_type=jnp.float32).astype(jnp.bfloat16)
            projected = lax.psum(proj_part, "col")
            state_mid = (state.astype(jnp.float32) + (projected.astype(jnp.float32) + b_o[layer].astype(jnp.float32))).astype(jnp.bfloat16)
            normed_two = layer_norm(state_mid, ln2_g[layer], ln2_b[layer])
            inner_part = jnp.dot(normed_two, w_fc1[layer], preferred_element_type=jnp.float32).astype(jnp.bfloat16)
            inner_sum = lax.psum(inner_part, "row")
            inner = jnp.maximum((inner_sum.astype(jnp.float32) + b_fc1[layer].astype(jnp.float32)).astype(jnp.bfloat16), 0)
            out_part = jnp.dot(inner, w_fc2[layer], preferred_element_type=jnp.float32).astype(jnp.bfloat16)
            out_sum = lax.psum(out_part, "col")
            state = (state_mid.astype(jnp.float32) + (out_sum.astype(jnp.float32) + b_fc2[layer].astype(jnp.float32))).astype(jnp.bfloat16)
            k_rows.append(k_fresh)
            v_rows.append(v_fresh)
        return state, jnp.stack(k_rows), jnp.stack(v_rows)

    return jax.shard_map(local_step, mesh=mesh, in_specs=in_specs,
                         out_specs=(act_spec, fresh_spec, fresh_spec), check_vma=False)
```

profile of v0, /device:TPU:0, one launch (start us, length us, event | category | flops | bytes accessed | tf_op | source)
XLA Modules:
  0.0 401.9 jit_solution(11938141747377106052)
XLA Ops:
  7.3 1.1 convert_reduce_fusion.3
  8.4 8.4 %psum.70 = f32[128,2]{0,1:T(2,128)S(1)} all-reduce(f32[128,2]{0,1:T(2,128)S(1)} %pad_maximum_fusion.2), channel_id=1, replica_groups=mesh['dp'=2,'col'=4,'row'=4] {'row'}, use_global_device_ids=true, to_apply=%region_2.0 | all-reduce | flops 256 | bytes 2048 | tf_op jit(solution)/shard_map/psum | solution.py:41
  18.4 1.8 convolution_convert_fusion.10
  20.3 1.8 convolution_convert_fusion.11
  22.2 1.9 convolution_convert_fusion.9
  28.9 11.4 %reduce-scatter.9.cloned.1.call-done = bf16[128,64]{0,1:T(8,128)(2,1)} async-done(((bf16[128,256]{0,1:T(8,128)(2,1)}), bf16[128,64]{0,1:T(8,128)(2,1)}) %reduce-scatter.9.cloned.1.call-update) | async-done | bytes 16400 | tf_op jit(solution)/shard_map/reduce_scatter | solution.py:50
  40.3 22.0 %reduce-scatter.7.cloned.1.call-done = bf16[128,64]{0,1:T(8,128)(2,1)} async-done(((bf16[128,256]{0,1:T(8,128)(2,1)}), bf16[128,64]{0,1:T(8,128)(2,1)}) %reduce-scatter.7.cloned.1.call-update) | async-done | bytes 16400 | tf_op jit(solution)/shard_map/reduce_scatter | solution.py:50
  63.3 4.6 %fusion.6 = f32[128,1,512]{2,1,0:T(1,128)S(1)} fusion(bf16[128,64,1]{1,2,0:T(2,128)(2,1)S(1)} %copy.23, bf16[2,128,1,512,64]{3,4,2,1,0:T(8,128)(2,1)} %param.22), kind=kOutput, calls=%fused_computation.6 | convolution fusion | flops 8388608 | bytes 8667136 | tf_op jit(solution)/shard_map/bhd,bhsd->bhs/dot_general | solution.py:10
  70.4 5.6 %fusion.4 = f32[128,1,64]{2,1,0:T(1,128)S(1)} fusion(bf16[2,128,1,512,64]{3,4,2,1,0:T(8,128)(2,1)} %param.23, bf16[128,512,1]{1,0,2:T(8,128)(2,1)S(1)} %fusion.74), kind=kOutput, calls=%fused_computation.4 | convolution fusion | flops 8388608 | bytes 8552448 | tf_op jit(solution)/shard_map/bhs,bhsd->bhd/dot_general | solution.py:20
  76.1 8.8 %reduce-scatter.11.cloned.1.call-done = bf16[128,64]{0,1:T(8,128)(2,1)} async-done(((bf16[128,256]{0,1:T(8,128)(2,1)}), bf16[128,64]{0,1:T(8,128)(2,1)}) %reduce-scatter.11.cloned.1.call-update) | async-done | bytes 16400 | tf_op jit(solution)/shard_map/reduce_scatter | solution.py:50
  85.7 5.2 %all_gather.6 = bf16[128,256]{0,1:T(8,128)(2,1)S(1)} all-gather(bf16[128,64]{0,1:T(8,128)(2,1)S(1)} %get-tuple-element.15), channel_id=1, replica_groups=mesh['dp'=2,'col'=4,'row'=4] {'row'}, dimensions={1}, use_global_device_ids=true | all-gather | bytes 81920 | tf_op jit(solution)/shard_map/all_gather | solution.py:70
  91.9 34.4 %all-reduce.7.cloned.1.call-done = bf16[128,256]{1,0:T(8,128)(2,1)} async-done(((bf16[128,256]{1,0:T(8,128)(2,1)}), bf16[128,256]{1,0:T(8,128)(2,1)}) %all-reduce.7.cloned.1.call-update) | async-done | bytes 65552 | tf_op jit(solution)/shard_map/psum | solution.py:72
  126.2 1.0 convert_reduce_fusion.2
  127.2 5.7 %psum.72 = f32[128,2]{0,1:T(2,128)S(1)} all-reduce(f32[128,2]{0,1:T(2,128)S(1)} %pad_maximum_fusion.3), channel_id=1, replica_groups=mesh['dp'=2,'col'=4,'row'=4] {'row'}, use_global_device_ids=true, to_apply=%region_11.12 | all-reduce | flops 256 | bytes 2048 | tf_op jit(solution)/shard_map/psum | solution.py:41
  132.9 1.0 convolution_convert_fusion.1
  134.0 32.2 %all-reduce.9.cloned.1.call-done = bf16[128,1024]{1,0:T(8,128)(2,1)} async-done(((bf16[128,1024]{1,0:T(8,128)(2,1)}), bf16[128,1024]{1,0:T(8,128)(2,1)}) %all-reduce.9.cloned.1.call-update) | async-done | bytes 262160 | tf_op jit(solution)/shard_map/psum | solution.py:76
  166.2 1.8 convolution_convert_fusion.3
  168.2 35.1 %all-reduce.11.cloned.1.call-done = bf16[128,256]{1,0:T(8,128)(2,1)} async-done(((bf16[128,256]{1,0:T(8,128)(2,1)}), bf16[128,256]{1,0:T(8,128)(2,1)}) %all-reduce.11.cloned.1.call-update) | async-done | bytes 65552 | tf_op jit(solution)/shard_map/psum | solution.py:79
  204.2 5.7 %psum.75 = f32[128,2]{0,1:T(2,128)S(1)} all-reduce(f32[128,2]{0,1:T(2,128)S(1)} %pad_maximum_fusion.4), channel_id=1, replica_groups=mesh['dp'=2,'col'=4,'row'=4] {'row'}, use_global_device_ids=true, to_apply=%region_16.17 | all-reduce | flops 256 | bytes 2048 | tf_op jit(solution)/shard_map/psum | solution.py:41
  212.9 17.7 %reduce-scatter.15.cloned.1.call-done = bf16[128,64]{0,1:T(8,128)(2,1)} async-done(((bf16[128,256]{0,1:T(8,128)(2,1)}), bf16[128,64]{0,1:T(8,128)(2,1)}) %reduce-scatter.15.cloned.1.call-update) | async-done | bytes 16400 | tf_op jit(solution)/shard_map/reduce_scatter | solution.py:50
  230.6 22.0 %reduce-scatter.13.cloned.1.call-done = bf16[128,64]{0,1:T(8,128)(2,1)} async-done(((bf16[128,256]{0,1:T(8,128)(2,1)}), bf16[128,64]{0,1:T(8,128)(2,1)}) %reduce-scatter.13.cloned.1.call-update) | async-done | bytes 16400 | tf_op jit(solution)/shard_map/reduce_scatter | solution.py:50
  253.6 4.6 %fusion.2 = f32[128,1,512]{2,1,0:T(1,128)S(1)} fusion(bf16[128,64,1]{1,2,0:T(2,128)(2,1)S(1)} %copy.30, bf16[2,128,1,512,64]{3,4,2,1,0:T(8,128)(2,1)} %param.22), kind=kOutput, calls=%fused_computation.2 | convolution fusion | flops 8388608 | bytes 8667136 | tf_op jit(solution)/shard_map/bhd,bhsd->bhs/dot_general | solution.py:10
  258.7 5.6 %fusion = f32[128,1,64]{2,1,0:T(1,128)S(1)} fusion(bf16[2,128,1,512,64]{3,4,2,1,0:T(8,128)(2,1)} %param.23, bf16[128,512,1]{1,0,2:T(8,128)(2,1)S(1)} %fusion.75), kind=kOutput, calls=%fused_computation | convolution fusion | flops 8388608 | bytes 8552448 | tf_op jit(solution)/shard_map/bhs,bhsd->bhd/dot_general | solution.py:20
  264.4 10.7 %reduce-scatter.17.cloned.1.call-done = bf16[128,64]{0,1:T(8,128)(2,1)} async-done(((bf16[128,256]{0,1:T(8,128)(2,1)}), bf16[128,64]{0,1:T(8,128)(2,1)}) %reduce-scatter.17.cloned.1.call-update) | async-done | bytes 16400 | tf_op jit(solution)/shard_map/reduce_scatter | solution.py:50
  276.0 5.2 %all_gather.7 = bf16[128,256]{0,1:T(8,128)(2,1)S(1)} all-gather(bf16[128,64]{0,1:T(8,128)(2,1)S(1)} %get-tuple-element.17), channel_id=1, replica_groups=mesh['dp'=2,'col'=4,'row'=4] {'row'}, dimensions={1}, use_global_device_ids=true | all-gather | bytes 81920 | tf_op jit(solution)/shard_map/all_gather | solution.py:70
  282.1 34.4 %all-reduce.13.cloned.1.call-done = bf16[128,256]{1,0:T(8,128)(2,1)} async-done(((bf16[128,256]{1,0:T(8,128)(2,1)}), bf16[128,256]{1,0:T(8,128)(2,1)}) %all-reduce.13.cloned.1.call-update) | async-done | bytes 65552 | tf_op jit(solution)/shard_map/psum | solution.py:72
  317.5 5.7 %psum.77 = f32[128,2]{0,1:T(2,128)S(1)} all-reduce(f32[128,2]{0,1:T(2,128)S(1)} %pad_maximum_fusion.5), channel_id=1, replica_groups=mesh['dp'=2,'col'=4,'row'=4] {'row'}, use_global_device_ids=true, to_apply=%region_25.26 | all-reduce | flops 256 | bytes 2048 | tf_op jit(solution)/shard_map/psum | solution.py:41
  323.2 1.0 convolution_convert_fusion
  324.8 31.6 %all-reduce.15.cloned.1.call-done = bf16[128,1024]{1,0:T(8,128)(2,1)} async-done(((bf16[128,1024]{1,0:T(8,128)(2,1)}), bf16[128,1024]{1,0:T(8,128)(2,1)}) %all-reduce.15.cloned.1.call-update) | async-done | bytes 262160 | tf_op jit(solution)/shard_map/psum | solution.py:76
  356.5 1.8 convolution_convert_fusion.2
  358.9 34.6 %all-reduce.17.cloned.1.call-done = bf16[128,256]{1,0:T(8,128)(2,1)} async-done(((bf16[128,256]{1,0:T(8,128)(2,1)}), bf16[128,256]{1,0:T(8,128)(2,1)}) %all-reduce.17.cloned.1.call-update) | async-done | bytes 65552 | tf_op jit(solution)/shard_map/psum | solution.py:79
  393.6 1.5 fusion.55
  (93 shorter events, 21.5 us)
Async XLA Ops:
  7.2 119.0 %copy-start = (bf16[128,256]{1,0:T(8,128)(2,1)S(1)}, bf16[128,256]{1,0:T(8,128)(2,1)}, u32[]{:S(2)}) copy-start(bf16[128,256]{1,0:T(8,128)(2,1)} %param.20) | copy-start | bytes 196612
  7.2 202.7 %copy-start.7 = (bf16[2,256,256]{2,1,0:T(8,128)(2,1)S(1)}, bf16[2,256,256]{2,1,0:T(8,128)(2,1)}, u32[]{:S(2)}) copy-start(bf16[2,256,256]{2,1,0:T(8,128)(2,1)} %param.28) | copy-start | bytes 786436
  7.2 203.7 %copy-start.8 = (bf16[2,256,256]{2,1,0:T(8,128)(2,1)S(1)}, bf16[2,256,256]{2,1,0:T(8,128)(2,1)}, u32[]{:S(2)}) copy-start(bf16[2,256,256]{2,1,0:T(8,128)(2,1)} %param.26) | copy-start | bytes 786436
  7.2 204.7 %copy-start.9 = (bf16[2,256,256]{2,1,0:T(8,128)(2,1)S(1)}, bf16[2,256,256]{2,1,0:T(8,128)(2,1)}, u32[]{:S(2)}) copy-start(bf16[2,256,256]{2,1,0:T(8,128)(2,1)} %param.30) | copy-start | bytes 786436
  7.2 83.7 %copy-start.1 = (bf16[2,256,256]{2,1,0:T(8,128)(2,1)S(1)}, bf16[2,256,256]{2,1,0:T(8,128)(2,1)}, u32[]{:S(2)}) copy-start(bf16[2,256,256]{2,1,0:T(8,128)(2,1)} %param.32) | copy-start | bytes 786436
  7.2 84.6 %copy-start.3 = (bf16[2,256]{1,0:T(2,128)(2,1)S(1)}, bf16[2,256]{1,0:T(2,128)(2,1)}, u32[]{:S(2)}) copy-start(bf16[2,256]{1,0:T(2,128)(2,1)} %param.35) | copy-start | bytes 3076
  7.2 125.6 %copy-start.5 = (bf16[2,256,1024]{2,1,0:T(8,128)(2,1)S(1)}, bf16[2,256,1024]{2,1,0:T(8,128)(2,1)}, u32[]{:S(2)}) copy-start(bf16[2,256,1024]{2,1,0:T(8,128)(2,1)} %param.36) | copy-start | bytes 3145732
  7.2 126.7 %copy-start.4 = (bf16[2,256]{1,0:T(2,128)(2,1)S(1)}, bf16[2,256]{1,0:T(2,128)(2,1)}, u32[]{:S(2)}) copy-start(bf16[2,256]{1,0:T(2,128)(2,1)} %param.39) | copy-start | bytes 3076
  7.3 158.9 %copy-start.6 = (bf16[2,1024,256]{2,1,0:T(8,128)(2,1)S(1)}, bf16[2,1024,256]{2,1,0:T(8,128)(2,1)}, u32[]{:S(2)}) copy-start(bf16[2,1024,256]{2,1,0:T(8,128)(2,1)} %param.38) | copy-start | bytes 3145732
  7.3 33.0 %reduce-scatter.9.cloned.1.call-start = ((), (), s32[]{:S(2)}) async-start(), calls=%async_computation.7 | async-start | bytes 81920 | tf_op jit(solution)/shard_map/reduce_scatter | solution.py:50
  20.3 42.0 %reduce-scatter.7.cloned.1.call-start = ((), (), s32[]{:S(2)}) async-start(), calls=%async_computation.6 | async-start | bytes 81920 | tf_op jit(solution)/shard_map/reduce_scatter | solution.py:50
  22.2 235.9 %copy-start.2 = (s32[128]{0:T(128)S(1)}, s32[128]{0:T(128)}, u32[]{:S(2)}) copy-start(s32[128]{0:T(128)} %param.21) | copy-start | bytes 1540
  22.2 62.7 %reduce-scatter.11.cloned.1.call-start = ((), (), s32[]{:S(2)}) async-start(), calls=%async_computation.8 | async-start | bytes 81920 | tf_op jit(solution)/shard_map/reduce_scatter | solution.py:50
  24.1 102.1 %all-reduce.7.cloned.1.call-start = ((), (), s32[]{:S(2)}) async-start(), calls=%async_computation.9 | async-start | bytes 131072 | tf_op jit(solution)/shard_map/psum | solution.py:72
  91.8 74.4 %all-reduce.9.cloned.1.call-start = ((), (), s32[]{:S(2)}) async-start(), calls=%async_computation.10 | async-start | bytes 524288 | tf_op jit(solution)/shard_map/psum | solution.py:76
  133.9 69.4 %all-reduce.11.cloned.1.call-start = ((), (), s32[]{:S(2)}) async-start(), calls=%async_computation.11 | async-start | bytes 131072 | tf_op jit(solution)/shard_map/psum | solution.py:79
  168.0 62.5 %reduce-scatter.15.cloned.1.call-start = ((), (), s32[]{:S(2)}) async-start(), calls=%async_computation.13 | async-start | bytes 81920 | tf_op jit(solution)/shard_map/reduce_scatter | solution.py:50
  210.9 41.7 %reduce-scatter.13.cloned.1.call-start = ((), (), s32[]{:S(2)}) async-start(), calls=%async_computation.12 | async-start | bytes 81920 | tf_op jit(solution)/shard_map/reduce_scatter | solution.py:50
  211.8 63.4 %reduce-scatter.17.cloned.1.call-start = ((), (), s32[]{:S(2)}) async-start(), calls=%async_computation.14 | async-start | bytes 81920 | tf_op jit(solution)/shard_map/reduce_scatter | solution.py:50
  212.8 103.7 %all-reduce.13.cloned.1.call-start = ((), (), s32[]{:S(2)}) async-start(), calls=%async_computation.15 | async-start | bytes 131072 | tf_op jit(solution)/shard_map/psum | solution.py:72
  282.1 74.4 %all-reduce.15.cloned.1.call-start = ((), (), s32[]{:S(2)}) async-start(), calls=%async_computation.16 | async-start | bytes 524288 | tf_op jit(solution)/shard_map/psum | solution.py:76
  324.2 69.4 %all-reduce.17.cloned.1.call-start = ((), (), s32[]{:S(2)}) async-start(), calls=%async_computation.17 | async-start | bytes 131072 | tf_op jit(solution)/shard_map/psum | solution.py:79
Sparse Core Ops, SparseCore 0:
  20.4 19.8 reduce-scatter.8
  42.7 19.5 reduce-scatter.6
  65.3 19.5 reduce-scatter.10
  91.9 34.2 all-reduce.6
  134.0 32.1 all-reduce.8
  168.9 34.2 all-reduce.10
  211.0 19.5 reduce-scatter.14
  233.0 19.5 reduce-scatter.12
  255.6 19.5 reduce-scatter.16
  282.2 34.2 all-reduce.12
  324.3 32.1 all-reduce.14
  359.2 34.2 all-reduce.16
where the time goes:
time: 403 us; the launch traced here: 402 us
  waiting for transfers between devices  295 us (73%)
  blocking collectives  35.9 us (9%)
  matrix products  35.9 us (9%)
  other arithmetic  17.2 us (4%)
  between operations  14.5 us (4%)
    reduce_scatter x6, waiting for transfers between devices, head_projection(): summed = lax.psum_scatter(partial, 'row', scatter_dimension=1, tiled=True)  92.6 us
    psum x2, waiting for transfers between devices, local_step(): out_sum = lax.psum(out_part, 'col')  69.7 us
    psum x2, waiting for transfers between devices, local_step(): projected = lax.psum(proj_part, 'col')  68.7 us
    psum x2, waiting for transfers between devices, local_step(): inner_sum = lax.psum(inner_part, 'row')  63.8 us
    psum x4, blocking collectives, layer_norm(): stats = lax.psum(stats, 'row')  25.4 us
    dot_general x2, matrix products, attention(): jnp.einsum('bhs,bhsd->bhd', prob_cache, v_layer, preferred_element_type=j...  11.3 us
    all_gather x2, blocking collectives, local_step(): lax.all_gather(attended.reshape(batch_rows, heads_dev * head_dim), 'row',...  10.5 us
    dot_general x2, matrix products, attention(): jnp.einsum('bhd,bhsd->bhs', q_heads, k_layer, preferred_element_type=jnp....  9.14 us
  transfers between devices with their start and end apart: 12, of which 12 were waited for; matrix products, arithmetic and copies ran while one was open for 9% of the time, Pallas kernels for 0%

commit v1 on v0

v1 whole, which is shorter than its diff:
```python
import functools

import jax
import jax.numpy as jnp
from jax import lax
from jax.experimental import pallas as pl
from jax.experimental.pallas import tpu as pltpu
from jax.sharding import PartitionSpec as P

EPS_LN = 1e-5
MESH = pl.DeviceIdType.MESH
F32 = jnp.float32
BF16 = jnp.bfloat16

LAYERS = 2
BATCH = 128
STREAMS = 2
ROWS = BATCH // STREAMS
HALF = ROWS // 2
GROUP = 16
N_ROW = 4
N_COL = 4
HEAD = 64
SEQ = 512
WIDTH = 256
D_MODEL = 1024
FF_LOC = 1024

VEC_NAMES = ("g1", "b1", "bq", "bk", "bv", "bo", "g2", "b2", "bf2")
MAT_NAMES = ("wq", "wk", "wv", "wo", "wf1", "wf2")


def lane_iota(shape):
    return lax.broadcasted_iota(jnp.int32, shape, len(shape) - 1)


def swap_halves(val):
    return pltpu.roll(val, HEAD, 1)


def low_half(shape):
    return lane_iota(shape) < HEAD


def step_kernel(*refs):
    (x_in, len_in, k_in, v_in, g1_in, b1_in, wq_in, bq_in, wk_in, bk_in, wv_in, bv_in,
     wo_in, bo_in, g2_in, b2_in, wf1_in, bf1_in, wf2_in, bf2_in,
     h_out, k_out, v_out,
     x_buf, len_buf, k_buf, v_buf, g1, b1, wq, bq, wk, bk, wv, bv, wo, bo, g2, b2, wf1, bf1, wf2, bf2,
     len_mat, kf_buf, vf_buf, s_buf, p_buf, o_mix,
     st_send, st_recv, gb_send, gb_recv, qkv_send, qkv_recv, o_recv, proj_recv, f1_send, f1_recv, u_recv, out_recv,
     load_sem, big_sem, store_sem, send_sem, recv_sem) = refs

    row = lax.axis_index("row")
    col = lax.axis_index("col")

    loads = {}

    def load(name, src, dst, sem):
        copy = pltpu.make_async_copy(src, dst, sem)
        copy.start()
        loads[name] = copy

    n_load = [0]

    def small(name, src, dst):
        load(name, src, dst, load_sem.at[n_load[0]])
        n_load[0] += 1

    small("x", x_in, x_buf)
    small("g1", g1_in, g1)
    for layer in range(LAYERS):
        for name, src, dst in (("wq", wq_in, wq), ("wk", wk_in, wk), ("wv", wv_in, wv)):
            if layer == 0:
                small((name, layer), src.at[layer], dst.at[layer])
    for name, src, dst in (("b1", b1_in, b1), ("bq", bq_in, bq), ("bk", bk_in, bk), ("bv", bv_in, bv),
                           ("len", len_in, len_buf), ("bo", bo_in, bo), ("g2", g2_in, g2), ("b2", b2_in, b2),
                           ("bf1", bf1_in, bf1), ("bf2", bf2_in, bf2)):
        small(name, src, dst)

    barrier = pltpu.get_barrier_semaphore()
    for off in range(1, 4):
        pl.semaphore_signal(barrier, inc=1, device_id={"row": lax.rem(row + off, N_ROW)}, device_id_type=MESH)
        pl.semaphore_signal(barrier, inc=1, device_id={"col": lax.rem(col + off, N_COL)}, device_id_type=MESH)

    def big(layer, stream, which):
        src, dst = (k_in, k_buf) if which == 0 else (v_in, v_buf)
        span = pl.ds(stream * ROWS * HEAD, ROWS * HEAD)
        load(("kv", layer, stream, which), src.at[layer, span], dst.at[layer, span],
             big_sem.at[(layer * STREAMS + stream) * 2 + which])

    for stream in range(STREAMS):
        for which in range(2):
            big(0, stream, which)
    for name, src, dst in (("wo", wo_in, wo), ("wf1", wf1_in, wf1), ("wf2", wf2_in, wf2)):
        small((name, 0), src.at[0], dst.at[0])
    for name, src, dst in (("wq", wq_in, wq), ("wk", wk_in, wk), ("wv", wv_in, wv), ("wo", wo_in, wo),
                           ("wf1", wf1_in, wf1), ("wf2", wf2_in, wf2)):
        small((name, 1), src.at[1], dst.at[1])
    for stream in range(STREAMS):
        for which in range(2):
            big(1, stream, which)

    waited = set()

    def need(name):
        if name not in waited:
            waited.add(name)
            loads[name].wait()

    sends = []
    recvs = {}
    n_sem = [0]

    def exchange(tag, axis, src_of, dst_of):
        me = row if axis == "row" else col
        waits = []
        for off in (2, 3, 1):
            dest = lax.rem(me + off, 4)
            source = lax.rem(me + 4 - off, 4)
            index = n_sem[0]
            n_sem[0] += 1
            out = pltpu.make_async_remote_copy(
                src_ref=src_of(dest), dst_ref=dst_of(me), send_sem=send_sem.at[index],
                recv_sem=recv_sem.at[index], device_id={axis: dest}, device_id_type=MESH)
            out.start()
            sends.append(out)
            waits.append(pltpu.make_async_remote_copy(
                src_ref=src_of(dest), dst_ref=dst_of(source), send_sem=send_sem.at[index],
                recv_sem=recv_sem.at[index], device_id={axis: dest}, device_id_type=MESH))
        recvs[tag] = waits

    def arrived(tag):
        for copy in recvs[tag]:
            copy.wait_recv()

    def local_norm(state, gain):
        mean = jnp.sum(state, axis=-1, keepdims=True) * (1.0 / WIDTH)
        delta = state - mean
        var = jnp.sum(delta * delta, axis=-1, keepdims=True) * (1.0 / WIDTH)
        normed = (delta * lax.rsqrt(var + EPS_LN) * gain).astype(BF16)
        lanes = lane_iota((ROWS, 128))
        tile = jnp.where(lanes == 0, mean, jnp.where(lanes == 1, var, 0.0))
        if ROWS < 128:
            tile = jnp.concatenate([tile] * (128 // ROWS), axis=0)
        return normed, jnp.transpose(tile)[0:8]

    def stat_columns(stats):
        means = [stats[r, 0:1] for r in range(N_ROW)]
        variances = [stats[r, 1:2] for r in range(N_ROW)]
        mean = (means[0] + means[1] + means[2] + means[3]) * 0.25
        gaps = [m - mean for m in means]
        var = (variances[0] + variances[1] + variances[2] + variances[3]
               + gaps[0] * gaps[0] + gaps[1] * gaps[1] + gaps[2] * gaps[2] + gaps[3] * gaps[3]) * 0.25
        inv = lax.rsqrt(var + EPS_LN)
        lines = [jnp.sqrt(v + EPS_LN) * inv for v in variances] + [g * inv for g in gaps]
        sub = lax.broadcasted_iota(jnp.int32, (8, 128), 0)
        tile = jnp.zeros((8, 128), F32)
        for i, line in enumerate(lines):
            tile = jnp.where(sub == i, line, tile)
        turned = jnp.transpose(jnp.concatenate([tile] * 16, axis=0))[0:ROWS]
        return [turned[:, i:i + 1] for i in range(8)]

    def pack_heads(q, k, v, j, rows):
        half = rows // 2
        lo = (j // 2) * 128
        q, k, v = q[:, lo:lo + 128], k[:, lo:lo + 128], v[:, lo:lo + 128]
        if j % 2 == 0:
            first = jnp.where(low_half((rows, 128)), q, swap_halves(k))
            second = jnp.where(low_half((half, 128)), v[:half], swap_halves(v[half:]))
        else:
            first = jnp.where(low_half((rows, 128)), swap_halves(q), k)
            second = jnp.where(low_half((half, 128)), swap_halves(v[:half]), v[half:])
        return first, second

    def dot(a, b):
        return jnp.dot(a, b, preferred_element_type=F32)

    def send_qkv(layer, stream):
        slot = layer * STREAMS + stream
        need("x")
        need("g1")
        state = x_buf[stream * ROWS:(stream + 1) * ROWS, :].astype(F32)
        normed, tile = local_norm(state, g1[layer:layer + 1, :].astype(F32))
        st_send[2 * slot] = tile
        st_recv[2 * slot, row] = tile
        for name in ("wq", "wk", "wv"):
            need((name, layer))
        q, k, v = dot(normed, wq[layer]), dot(normed, wk[layer]), dot(normed, wv[layer])
        for j in range(N_ROW):
            first, second = pack_heads(q, k, v, j, ROWS)
            qkv_send[slot, j, 0:ROWS] = first.astype(BF16)
            qkv_send[slot, j, ROWS:ROWS + HALF] = second.astype(BF16)
        qkv_recv[slot, row] = qkv_send[slot, row]
        if layer == 0 and stream == 0:
            pl.semaphore_wait(barrier, 6)
        exchange(("st1", slot), "row", lambda d: st_send.at[2 * slot], lambda s: st_recv.at[2 * slot, s])
        exchange(("qkv", slot), "row", lambda d: qkv_send.at[slot, d], lambda s: qkv_recv.at[slot, s])

    def affine_rows(gain, shift):
        sub = lax.broadcasted_iota(jnp.int32, (16, WIDTH), 0)
        return jnp.where(sub == 0, gain.astype(F32), jnp.where(sub == 1, shift.astype(F32), 0.0)).astype(BF16)

    def send_affine(layer, kind):
        slot = layer * 2 + kind
        bias_on = jnp.where(row == 0, 1.0, 0.0)
        sub = lax.broadcasted_iota(jnp.int32, (8, 128), 0)
        if kind == 0:
            for name in ("b1", "bq", "bk", "bv"):
                need(name)
            rows = affine_rows(g1[layer:layer + 1, :], b1[layer:layer + 1, :])
            parts = []
            for w, b in ((wq, bq), (wk, bk), (wv, bv)):
                bias = b[layer:layer + 1, :].astype(F32) * bias_on
                part = dot(rows, w[layer])[0:8]
                sub_w = lax.broadcasted_iota(jnp.int32, (8, WIDTH), 0)
                parts.append(part + jnp.where(sub_w == 1, bias, 0.0))
            q, k, v = parts
            for j in range(N_ROW):
                lo = (j // 2) * 128
                qj, kj, vj = q[:, lo:lo + 128], k[:, lo:lo + 128], v[:, lo:lo + 128]
                if j % 2 == 0:
                    first = jnp.where(low_half((8, 128)), qj, swap_halves(kj))
                    second = jnp.where(low_half((8, 128)), vj, swap_halves(vj))
                else:
                    first = jnp.where(low_half((8, 128)), swap_halves(qj), kj)
                    second = jnp.where(low_half((8, 128)), swap_halves(vj), vj)
                gb_send[slot, j] = jnp.concatenate([first, second], axis=1)
        else:
            for name in ("g2", "b2", "bf1", ("wf1", layer)):
                need(name)
            rows = affine_rows(g2[layer:layer + 1, :], b2[layer:layer + 1, :])
            part = dot(rows, wf1[layer])[0:8]
            sub_w = lax.broadcasted_iota(jnp.int32, (8, FF_LOC), 0)
            part = part + jnp.where(sub_w == 1, bf1[layer:layer + 1, :].astype(F32) * bias_on, 0.0)
            for j in range(N_ROW):
                gb_send[slot, j] = part[:, j * WIDTH:(j + 1) * WIDTH]
        gb_recv[slot, row] = gb_send[slot, row]
        exchange(("gb", slot), "row", lambda d: gb_send.at[slot, d], lambda s: gb_recv.at[slot, s])

    gb_done = set()

    def affine_lines(layer, kind):
        slot = layer * 2 + kind
        if slot not in gb_done:
            gb_done.add(slot)
            arrived(("gb", slot))
        tiles = [gb_recv[slot, r] for r in range(N_ROW)]
        gains = [t[0:1] for t in tiles]
        const = tiles[0][1:2] + tiles[1][1:2] + tiles[2][1:2] + tiles[3][1:2]
        return gains, const

    def attend(layer, stream):
        slot = layer * STREAMS + stream
        span = slice(stream * ROWS, (stream + 1) * ROWS)
        arrived(("st1", slot))
        cols = stat_columns(st_recv[2 * slot])
        gains, const = affine_lines(layer, 0)
        arrived(("qkv", slot))
        low = low_half((HALF, 128))
        qk = const[:, 0:128]
        vv = const[:, 128:256]
        for r in range(N_ROW):
            part = qkv_recv[slot, r].astype(F32)
            scale, shift = cols[r], cols[4 + r]
            qk = qk + part[0:ROWS] * scale + shift * gains[r][:, 0:128]
            scale_v = jnp.where(low, scale[0:HALF], scale[HALF:ROWS])
            shift_v = jnp.where(low, shift[0:HALF], shift[HALF:ROWS])
            vv = vv + part[ROWS:ROWS + HALF] * scale_v + shift_v * gains[r][:, 128:256]
        full_low = low_half((ROWS, 128))
        qk_turn = swap_halves(qk)
        q2 = (jnp.where(full_low, qk, qk_turn) * (HEAD ** -0.5)).astype(BF16)
        k2 = jnp.where(full_low, qk_turn, qk).astype(BF16)
        vv_turn = swap_halves(vv)
        v2 = jnp.concatenate([jnp.where(low, vv, vv_turn), jnp.where(low, vv_turn, vv)], axis=0).astype(BF16)
        kf_buf[layer, span, :] = k2[:, 0:HEAD]
        vf_buf[layer, span, :] = v2[:, 0:HEAD]
        score_new = jnp.sum(jnp.where(full_low, q2.astype(F32) * k2.astype(F32), 0.0), axis=-1, keepdims=True)

        need(("kv", layer, stream, 0))
        q_row = lax.broadcasted_iota(jnp.int32, (GROUP, 128), 0)
        q_half = lane_iota((GROUP, 128)) // HEAD
        for g in range(ROWS // GROUP):
            base = (stream * ROWS + g * GROUP) * HEAD
            qg = q2[g * GROUP:(g + 1) * GROUP].astype(F32)
            spread = [jnp.where(q_row == 2 * j + q_half, qg, 0.0).astype(BF16) for j in range(GROUP // 2)]
            s_buf[g * GROUP:(g + 1) * GROUP, :] = dot(jnp.concatenate(spread, axis=1),
                                                      k_buf[layer, base:base + GROUP * HEAD, :])
        positions = lane_iota((ROWS, SEQ)).astype(F32)
        limit = len_mat[span, 0:1]
        scores = jnp.where(positions < limit, s_buf[...], -jnp.inf)
        peak = jnp.maximum(jnp.max(scores, axis=-1, keepdims=True), score_new)
        exp_cache = jnp.exp(scores - peak)
        exp_new = jnp.exp(score_new - peak)
        inv = 1.0 / (jnp.sum(exp_cache, axis=-1, keepdims=True) + exp_new)
        p_buf[...] = (exp_cache * inv).astype(BF16)
        prob_new = (exp_new * inv).astype(BF16).astype(F32)

        need(("kv", layer, stream, 1))
        for g in range(ROWS // GROUP):
            base = (stream * ROWS + g * GROUP) * HEAD
            wide = lax.dot_general(p_buf[g * GROUP:(g + 1) * GROUP, :], v_buf[layer, base:base + GROUP * HEAD, :],
                                   (((1,), (1,)), ((), ())), preferred_element_type=F32)
            acc = jnp.zeros((GROUP, 128), F32)
            for j in range(GROUP // 2):
                acc = acc + jnp.where(q_row == 2 * j + q_half, wide[:, j * 128:(j + 1) * 128], 0.0)
            o_mix[g * GROUP:(g + 1) * GROUP, :] = acc + swap_halves(acc)
        o2 = o_mix[...] + prob_new * v2.astype(F32)
        o_recv[slot, row] = jnp.where(low, o2[0:HALF], o2[HALF:ROWS]).astype(BF16)
        exchange(("o", slot), "row", lambda d: o_recv.at[slot, row], lambda s: o_recv.at[slot, s])

    def project(layer, stream):
        slot = layer * STREAMS + stream
        need(("wo", layer))
        arrived(("o", slot))
        low = low_half((HALF, 128))
        parts = [o_recv[slot, r].astype(F32) for r in range(N_ROW)]
        turns = [swap_halves(p) for p in parts]
        pairs = []
        for a, b in ((0, 1), (2, 3)):
            top = jnp.where(low, parts[a], turns[b])
            bottom = jnp.where(low, turns[a], parts[b])
            pairs.append(jnp.concatenate([top, bottom], axis=0).astype(BF16))
        proj_recv[slot, col] = dot(jnp.concatenate(pairs, axis=1), wo[layer]).astype(BF16)
        exchange(("proj", slot), "col", lambda d: proj_recv.at[slot, col], lambda s: proj_recv.at[slot, s])

    def residual(slot, buf, bias, stream):
        span = slice(stream * ROWS, (stream + 1) * ROWS)
        total = buf[slot, 0].astype(F32)
        for c in range(1, N_COL):
            total = total + buf[slot, c].astype(F32)
        new = (x_buf[span, :].astype(F32) + (total + bias)).astype(BF16)
        x_buf[span, :] = new
        return new.astype(F32)

    def send_inner(layer, stream):
        slot = layer * STREAMS + stream
        need("bo")
        need("g2")
        need(("wf1", layer))
        arrived(("proj", slot))
        state = residual(slot, proj_recv, bo[layer:layer + 1, :].astype(F32), stream)
        normed, tile = local_norm(state, g2[layer:layer + 1, :].astype(F32))
        st_send[2 * slot + 1] = tile
        st_recv[2 * slot + 1, row] = tile
        exchange(("st2", slot), "row", lambda d: st_send.at[2 * slot + 1], lambda s: st_recv.at[2 * slot + 1, s])
        for j in range(N_ROW):
            f1_send[slot, j] = dot(normed, wf1[layer, :, j * WIDTH:(j + 1) * WIDTH]).astype(BF16)
        f1_recv[slot, row] = f1_send[slot, row]
        exchange(("f1", slot), "row", lambda d: f1_send.at[slot, d], lambda s: f1_recv.at[slot, s])

    def send_act(layer, stream):
        slot = layer * STREAMS + stream
        arrived(("st2", slot))
        cols = stat_columns(st_recv[2 * slot + 1])
        gains, const = affine_lines(layer, 1)
        arrived(("f1", slot))
        total = const
        for r in range(N_ROW):
            total = total + f1_recv[slot, r].astype(F32) * cols[r] + cols[4 + r] * gains[r]
        u_recv[slot, row] = jnp.maximum(total, 0.0).astype(BF16)
        exchange(("u", slot), "row", lambda d: u_recv.at[slot, row], lambda s: u_recv.at[slot, s])

    def send_out(layer, stream):
        slot = layer * STREAMS + stream
        need(("wf2", layer))
        arrived(("u", slot))
        acc = dot(u_recv[slot, 0], wf2[layer, 0:WIDTH, :])
        for r in range(1, N_ROW):
            acc = acc + dot(u_recv[slot, r], wf2[layer, r * WIDTH:(r + 1) * WIDTH, :])
        out_recv[slot, col] = acc.astype(BF16)
        exchange(("out", slot), "col", lambda d: out_recv.at[slot, col], lambda s: out_recv.at[slot, s])

    def finish(layer, stream):
        slot = layer * STREAMS + stream
        need("bf2")
        arrived(("out", slot))
        residual(slot, out_recv, bf2[layer:layer + 1, :].astype(F32), stream)

    stores = []

    def store(src, dst, index):
        copy = pltpu.make_async_copy(src, dst, store_sem.at[index])
        copy.start()
        stores.append(copy)

    for stream in range(STREAMS):
        send_qkv(0, stream)
    send_affine(0, 0)
    need("len")
    len_mat[...] = jnp.transpose(jnp.broadcast_to(len_buf[...].astype(F32), (128, 128)))
    for layer in range(LAYERS):
        for stream in range(STREAMS):
            attend(layer, stream)
        store(kf_buf.at[layer], k_out.at[layer], 2 * layer)
        store(vf_buf.at[layer], v_out.at[layer], 2 * layer + 1)
        if layer == 0:
            send_affine(0, 1)
        for stream in range(STREAMS):
            project(layer, stream)
        if layer == 0:
            for name in MAT_NAMES[:3]:
                need((name, 1))
            send_affine(1, 0)
            send_affine(1, 1)
        for stream in range(STREAMS):
            send_inner(layer, stream)
        for stream in range(STREAMS):
            send_act(layer, stream)
        for stream in range(STREAMS):
            send_out(layer, stream)
        for stream in range(STREAMS):
            finish(layer, stream)
            if layer + 1 < LAYERS:
                send_qkv(layer + 1, stream)
            else:
                span = pl.ds(stream * ROWS, ROWS)
                store(x_buf.at[span], h_out.at[span], 2 * LAYERS + stream)
    for copy in stores:
        copy.wait()
    for copy in sends:
        copy.wait_send()


N_SLOT = LAYERS * STREAMS
N_COPY = 3 * (8 * N_SLOT - 0 + 2 * LAYERS)


def run_step(x, lens, k_cache, v_cache, g1, b1, wq, bq, wk, bk, wv, bv, wo, bo, g2, b2, wf1, bf1, wf2, bf2):
    any_spec = pl.BlockSpec(memory_space=pl.ANY)
    args = (x, lens.reshape(1, BATCH),
            jnp.swapaxes(k_cache, 3, 4).reshape(LAYERS, BATCH * HEAD, SEQ),
            jnp.swapaxes(v_cache, 3, 4).reshape(LAYERS, BATCH * HEAD, SEQ),
            g1, b1, wq, bq, wk, bk, wv, bv, wo, bo, g2, b2, wf1, bf1, wf2, bf2)
    vm = pltpu.VMEM
    in_scratch = [vm(a.shape, a.dtype) for a in args]
    scratch = in_scratch + [
        vm((BATCH, 128), F32),
        vm((LAYERS, BATCH, HEAD), BF16),
        vm((LAYERS, BATCH, HEAD), BF16),
        vm((ROWS, SEQ), F32),
        vm((ROWS, SEQ), BF16),
        vm((ROWS, 128), F32),
        vm((2 * N_SLOT, 8, 128), F32),
        vm((2 * N_SLOT, N_ROW, 8, 128), F32),
        vm((2 * LAYERS, N_ROW, 8, WIDTH), F32),
        vm((2 * LAYERS, N_ROW, 8, WIDTH), F32),
        vm((N_SLOT, N_ROW, ROWS + HALF, 128), BF16),
        vm((N_SLOT, N_ROW, ROWS + HALF, 128), BF16),
        vm((N_SLOT, N_ROW, HALF, 128), BF16),
        vm((N_SLOT, N_COL, ROWS, WIDTH), BF16),
        vm((N_SLOT, N_ROW, ROWS, WIDTH), BF16),
        vm((N_SLOT, N_ROW, ROWS, WIDTH), BF16),
        vm((N_SLOT, N_ROW, ROWS, WIDTH), BF16),
        vm((N_SLOT, N_COL, ROWS, WIDTH), BF16),
        pltpu.SemaphoreType.DMA((32,)),
        pltpu.SemaphoreType.DMA((2 * N_SLOT,)),
        pltpu.SemaphoreType.DMA((2 * LAYERS + STREAMS,)),
        pltpu.SemaphoreType.DMA((N_COPY,)),
        pltpu.SemaphoreType.DMA((N_COPY,)),
    ]
    h_out, k_new, v_new = pl.pallas_call(
        step_kernel,
        out_shape=(jax.ShapeDtypeStruct((BATCH, WIDTH), BF16),
                   jax.ShapeDtypeStruct((LAYERS, BATCH, HEAD), BF16),
                   jax.ShapeDtypeStruct((LAYERS, BATCH, HEAD), BF16)),
        in_specs=[any_spec] * len(args),
        out_specs=(any_spec,) * 3,
        scratch_shapes=scratch,
        compiler_params=pltpu.CompilerParams(
            collective_id=0, has_side_effects=True, vmem_limit_bytes=60 * 1024 * 1024),
        name="decode_step",
    )(*args)
    return h_out, k_new.reshape(LAYERS, BATCH, 1, HEAD), v_new.reshape(LAYERS, BATCH, 1, HEAD)


def solution(mesh):
    act_spec = P("dp", "row")
    cache_spec = P(None, "dp", ("col", "row"), None, None)
    fresh_spec = P(None, "dp", ("col", "row"), None)
    in_weight = P(None, "row", "col")
    out_weight = P(None, "col", "row")
    col_vec = P(None, "col")
    row_vec = P(None, "row")
    in_specs = (act_spec, P("dp"), cache_spec, cache_spec, row_vec, row_vec,
                in_weight, col_vec, in_weight, col_vec, in_weight, col_vec,
                out_weight, row_vec, row_vec, row_vec, in_weight, col_vec, out_weight, row_vec)
    return jax.shard_map(run_step, mesh=mesh, in_specs=in_specs,
                         out_specs=(act_spec, fresh_spec, fresh_spec), check_vma=False)
```

time: 403 us -> 72.7 us (0.18)
  waiting for transfers between devices: 295 us -> 0 us
  Pallas kernels: 0 us -> 67.2 us
  matrix products: 35.9 us -> 0 us
  blocking collectives: 35.9 us -> 0 us
  other arithmetic: 17.2 us -> 0 us
  between operations: 14.5 us -> 0.65 us
    psum x6 -> x0, waiting for transfers between devices: 202 us -> none  [the longest x2 69.7 us: local_step(): out_sum = lax.psum(out_part, 'col')]
    reduce_scatter x6 -> x0, waiting for transfers between devices: 92.6 us -> none  [head_projection(): summed = lax.psum_scatter(partial, 'row', scatter_dimension=1, tiled=True)]
    pallas_call x0 -> x1, Pallas kernels: none -> 67.2 us  [run_step(): pl.pallas_call(step_kernel, out_shape=(jax.ShapeDtypeStruct((BATCH, WIDTH...]
    dot_general x16 -> x0, matrix products: 35.9 us -> none  [the longest x2 11.3 us: attention(): jnp.einsum('bhs,bhsd->bhd', prob_cache, v_layer, preferred_element_type=j...]
    psum x4 -> x0, blocking collectives: 25.4 us -> none  [layer_norm(): stats = lax.psum(stats, 'row')]
    all_gather x2 -> x0, blocking collectives: 10.5 us -> none  [local_step(): lax.all_gather(attended.reshape(batch_rows, heads_dev * head_dim), 'row',...]
    reduce_sum x6 -> x0, other arithmetic: 5.03 us -> none  [the longest x4 3.97 us: layer_norm(): jnp.sum(state_f32, axis=-1)]
    another operation x10 -> x0, other arithmetic: 4.53 us -> none  [the longest x6 4.49 us: local_step(): return (state, jnp.stack(k_rows), jnp.stack(v_rows))]
  transfers between devices with their start and end apart: 12 -> 0, of which waited for: 12 -> 0; matrix products, arithmetic and copies ran while one was open for 9% -> 0% of each run, Pallas kernels for 0% -> 0%
where the time goes in v1:
time: 72.7 us; the launch traced here: 72.4 us
  Pallas kernels  67.2 us (92%)
  local copies, waits for them, and re-layouts  4.55 us (6%)
    pallas_call x1, Pallas kernels, run_step(): pl.pallas_call(step_kernel, out_shape=(jax.ShapeDtypeStruct((BATCH, WIDTH...  67.2 us
    unnamed x3, local copies, waits for them, and re-layouts  4.55 us

profile of v1, /device:TPU:0, one launch (start us, length us, event | category | flops | bytes accessed | tf_op | source)
XLA Modules:
  0.0 72.4 jit_solution(11085478194543579750)
XLA Ops:
  0.6 67.2 %decode_step.1 = (bf16[128,256]{1,0:T(8,128)(2,1)}, bf16[2,128,64]{2,1,0:T(8,128)(2,1)}, bf16[2,128,64]{2,1,0:T(8,128)(2,1)}) custom-call(bf16[128,256]{1,0:T(8,128)(2,1)} %refs_0_.1, s32[1,128]{1,0:T(1,128)} %bitcast.13, bf16[2,8192,512]{2,1,0:T(8,128)(2,1)} %bitcast.9, bf16[2,8192,512]{2,1,0:T(8,128)(2,1)} %bitcast.10, bf16[2,256]{1,0:T(2,128)(2,1)} %refs_4_.1, ...), custom_call_target="tpu_custom_call" | custom-call | tf_op jit(solution)/shard_map/decode_step/pallas_call | solution.py:462
  67.9 1.5 %copy.23 = bf16[2,128,1,64]{1,3,2,0:T(8,128)(2,1)} copy(bf16[2,128,1,64]{3,1,0,2:T(8,128)(2,1)} %bitcast.12) | data formatting | bytes 65536
  69.4 1.5 %copy.24 = bf16[2,128,1,64]{1,3,2,0:T(8,128)(2,1)} copy(bf16[2,128,1,64]{3,1,0,2:T(8,128)(2,1)} %bitcast.11) | data formatting | bytes 65536
  71.0 1.5 %copy.26 = bf16[128,256]{1,0:T(8,128)(2,1)} copy(bf16[128,256]{1,0:T(8,128)(2,1)} %get-tuple-element.15) | data formatting | bytes 131072

commit v2 on v1

--- a/solution.py
+++ b/solution.py
@@ -14,7 +14,7 @@
 
 LAYERS = 2
 BATCH = 128
-STREAMS = 2
+STREAMS = 4
 ROWS = BATCH // STREAMS
 HALF = ROWS // 2
 GROUP = 16
@@ -47,7 +47,7 @@
      wo_in, bo_in, g2_in, b2_in, wf1_in, bf1_in, wf2_in, bf2_in,
      h_out, k_out, v_out,
      x_buf, len_buf, k_buf, v_buf, g1, b1, wq, bq, wk, bk, wv, bv, wo, bo, g2, b2, wf1, bf1, wf2, bf2,
-     len_mat, kf_buf, vf_buf, s_buf, p_buf, o_mix,
+     len_mat, kv_mix, kv_turn, s_buf, p_buf, o_mix,
      st_send, st_recv, gb_send, gb_recv, qkv_send, qkv_recv, o_recv, proj_recv, f1_send, f1_recv, u_recv, out_recv,
      load_sem, big_sem, store_sem, send_sem, recv_sem) = refs
 
@@ -273,8 +273,7 @@
         k2 = jnp.where(full_low, qk_turn, qk).astype(BF16)
         vv_turn = swap_halves(vv)
         v2 = jnp.concatenate([jnp.where(low, vv, vv_turn), jnp.where(low, vv_turn, vv)], axis=0).astype(BF16)
-        kf_buf[layer, span, :] = k2[:, 0:HEAD]
-        vf_buf[layer, span, :] = v2[:, 0:HEAD]
+        kv_mix[layer, span, :] = jnp.where(full_low, k2.astype(F32), v2.astype(F32))
         score_new = jnp.sum(jnp.where(full_low, q2.astype(F32) * k2.astype(F32), 0.0), axis=-1, keepdims=True)
 
         need(("kv", layer, stream, 0))
@@ -392,8 +391,9 @@
     for layer in range(LAYERS):
         for stream in range(STREAMS):
             attend(layer, stream)
-        store(kf_buf.at[layer], k_out.at[layer], 2 * layer)
-        store(vf_buf.at[layer], v_out.at[layer], 2 * layer + 1)
+        kv_turn[layer] = jnp.transpose(kv_mix[layer]).astype(BF16)
+        store(kv_turn.at[layer, 0:HEAD], k_out.at[layer], 2 * layer)
+        store(kv_turn.at[layer, HEAD:2 * HEAD], v_out.at[layer], 2 * layer + 1)
         if layer == 0:
             send_affine(0, 1)
         for stream in range(STREAMS):
@@ -426,6 +426,15 @@
 N_COPY = 3 * (8 * N_SLOT - 0 + 2 * LAYERS)
 
 
+def emit_kernel(h_in, k_in, v_in, h_out, k_out, v_out, sem):
+    copies = [pltpu.make_async_copy(src, dst, sem.at[i])
+              for i, (src, dst) in enumerate(((h_in, h_out), (k_in, k_out), (v_in, v_out)))]
+    for copy in copies:
+        copy.start()
+    for copy in copies:
+        copy.wait()
+
+
 def run_step(x, lens, k_cache, v_cache, g1, b1, wq, bq, wk, bk, wv, bv, wo, bo, g2, b2, wf1, bf1, wf2, bf2):
     any_spec = pl.BlockSpec(memory_space=pl.ANY)
     args = (x, lens.reshape(1, BATCH),
@@ -436,8 +445,8 @@
     in_scratch = [vm(a.shape, a.dtype) for a in args]
     scratch = in_scratch + [
         vm((BATCH, 128), F32),
-        vm((LAYERS, BATCH, HEAD), BF16),
-        vm((LAYERS, BATCH, HEAD), BF16),
+        vm((LAYERS, BATCH, 128), F32),
+        vm((LAYERS, BATCH, 128), BF16),
         vm((ROWS, SEQ), F32),
         vm((ROWS, SEQ), BF16),
         vm((ROWS, 128), F32),
@@ -459,19 +468,33 @@
         pltpu.SemaphoreType.DMA((N_COPY,)),
         pltpu.SemaphoreType.DMA((N_COPY,)),
     ]
-    h_out, k_new, v_new = pl.pallas_call(
+    shapes = (jax.ShapeDtypeStruct((BATCH, WIDTH), BF16),
+              jax.ShapeDtypeStruct((LAYERS, HEAD, BATCH), BF16),
+              jax.ShapeDtypeStruct((LAYERS, HEAD, BATCH), BF16))
+    results = pl.pallas_call(
         step_kernel,
-        out_shape=(jax.ShapeDtypeStruct((BATCH, WIDTH), BF16),
-                   jax.ShapeDtypeStruct((LAYERS, BATCH, HEAD), BF16),
-                   jax.ShapeDtypeStruct((LAYERS, BATCH, HEAD), BF16)),
-        in_specs=[any_spec] * len(args),
+        out_shape=shapes,
+        in_specs=[pl.BlockSpec(memory_space=pltpu.HBM)] * len(args),
         out_specs=(any_spec,) * 3,
         scratch_shapes=scratch,
         compiler_params=pltpu.CompilerParams(
             collective_id=0, has_side_effects=True, vmem_limit_bytes=60 * 1024 * 1024),
         name="decode_step",
     )(*args)
-    return h_out, k_new.reshape(LAYERS, BATCH, 1, HEAD), v_new.reshape(LAYERS, BATCH, 1, HEAD)
+    h_out, k_new, v_new = pl.pallas_call(
+        emit_kernel,
+        out_shape=shapes,
+        in_specs=[pl.BlockSpec(memory_space=pltpu.VMEM)] * 3,
+        out_specs=(pl.BlockSpec(memory_space=pltpu.HBM),) * 3,
+        scratch_shapes=[pltpu.SemaphoreType.DMA((3,))],
+        compiler_params=pltpu.CompilerParams(vmem_limit_bytes=1024 * 1024),
+        name="emit",
+    )(*results)
+
+    def fresh(rows):
+        return jnp.swapaxes(rows, 1, 2).reshape(LAYERS, BATCH, 1, HEAD)
+
+    return h_out, fresh(k_new), fresh(v_new)
 
 
 def solution(mesh):

time: 72.7 us -> 71.9 us (0.989)
  local copies, waits for them, and re-layouts: 4.55 us -> 2.35 us
  Pallas kernels: 67.2 us -> 68.6 us
    unnamed x3 -> x6, local copies, waits for them, and re-layouts: 4.55 us -> 2.35 us
    pallas_call x1 -> x2, Pallas kernels: 67.2 us -> 68.6 us  [the longest x1 67.9 us: run_step(): pl.pallas_call(step_kernel, out_shape=shapes, in_specs=[pl.BlockSpec(memo...]
where the time goes in v2:
time: 71.9 us; the launch traced here: 71.6 us
  Pallas kernels  68.6 us (95%)
  local copies, waits for them, and re-layouts  2.35 us (3%)
    pallas_call x1, Pallas kernels, run_step(): pl.pallas_call(step_kernel, out_shape=shapes, in_specs=[pl.BlockSpec(memo...  67.9 us
    unnamed x6, local copies, waits for them, and re-layouts  2.35 us

profile of v2, /device:TPU:0, one launch (start us, length us, event | category | flops | bytes accessed | tf_op | source)
XLA Modules:
  0.0 71.6 jit_solution(5593447841395772265)
XLA Ops:
  0.6 67.9 %decode_step.1 = (bf16[128,256]{1,0:T(8,128)(2,1)}, bf16[2,64,128]{2,1,0:T(8,128)(2,1)}, bf16[2,64,128]{2,1,0:T(8,128)(2,1)}) custom-call(bf16[128,256]{1,0:T(8,128)(2,1)} %refs_0_.1, s32[1,128]{1,0:T(1,128)} %bitcast.19, bf16[2,8192,512]{2,1,0:T(8,128)(2,1)} %bitcast.17, bf16[2,8192,512]{2,1,0:T(8,128)(2,1)} %bitcast.18, bf16[2,256]{1,0:T(2,128)(2,1)} %refs_4_.1, ...), custom_call_target="tpu_custom_call" | custom-call | tf_op jit(solution)/shard_map/decode_step/pallas_call | solution.py:474
  68.6 0.0 copy-start
  68.6 0.8 %copy-done = bf16[128,256]{1,0:T(8,128)(2,1)S(1)} copy-done((bf16[128,256]{1,0:T(8,128)(2,1)S(1)}, bf16[128,256]{1,0:T(8,128)(2,1)}, u32[]{:S(2)}) %copy-start) | copy-done | bytes 65560
  69.4 0.0 copy-start.1
  69.4 0.8 %copy-done.1 = bf16[2,64,128]{2,1,0:T(8,128)(2,1)S(1)} copy-done((bf16[2,64,128]{2,1,0:T(8,128)(2,1)S(1)}, bf16[2,64,128]{2,1,0:T(8,128)(2,1)}, u32[]{:S(2)}) %copy-start.1) | copy-done | bytes 32792
  70.2 0.0 copy-start.2
  70.2 0.8 %copy-done.2 = bf16[2,64,128]{2,1,0:T(8,128)(2,1)S(1)} copy-done((bf16[2,64,128]{2,1,0:T(8,128)(2,1)S(1)}, bf16[2,64,128]{2,1,0:T(8,128)(2,1)}, u32[]{:S(2)}) %copy-start.2) | copy-done | bytes 32792
  70.9 0.7 emit.1
Async XLA Ops:
  68.6 0.8 %copy-start = (bf16[128,256]{1,0:T(8,128)(2,1)S(1)}, bf16[128,256]{1,0:T(8,128)(2,1)}, u32[]{:S(2)}) copy-start(bf16[128,256]{1,0:T(8,128)(2,1)} %get-tuple-element.9.h_in) | copy-start | bytes 196612
  69.4 0.8 %copy-start.1 = (bf16[2,64,128]{2,1,0:T(8,128)(2,1)S(1)}, bf16[2,64,128]{2,1,0:T(8,128)(2,1)}, u32[]{:S(2)}) copy-start(bf16[2,64,128]{2,1,0:T(8,128)(2,1)} %get-tuple-element.10.k_in) | copy-start | bytes 98308
  70.2 0.8 %copy-start.2 = (bf16[2,64,128]{2,1,0:T(8,128)(2,1)S(1)}, bf16[2,64,128]{2,1,0:T(8,128)(2,1)}, u32[]{:S(2)}) copy-start(bf16[2,64,128]{2,1,0:T(8,128)(2,1)} %get-tuple-element.11.v_in) | copy-start | bytes 98308

commit v3 on v2

--- a/solution.py
+++ b/solution.py
@@ -14,7 +14,7 @@
 
 LAYERS = 2
 BATCH = 128
-STREAMS = 4
+STREAMS = 2
 ROWS = BATCH // STREAMS
 HALF = ROWS // 2
 GROUP = 16
@@ -25,6 +25,7 @@
 WIDTH = 256
 D_MODEL = 1024
 FF_LOC = 1024
+FF_HALF = FF_LOC // 2
 
 VEC_NAMES = ("g1", "b1", "bq", "bk", "bv", "bo", "g2", "b2", "bf2")
 MAT_NAMES = ("wq", "wk", "wv", "wo", "wf1", "wf2")
@@ -48,11 +49,16 @@
      h_out, k_out, v_out,
      x_buf, len_buf, k_buf, v_buf, g1, b1, wq, bq, wk, bk, wv, bv, wo, bo, g2, b2, wf1, bf1, wf2, bf2,
      len_mat, kv_mix, kv_turn, s_buf, p_buf, o_mix,
-     st_send, st_recv, gb_send, gb_recv, qkv_send, qkv_recv, o_recv, proj_recv, f1_send, f1_recv, u_recv, out_recv,
+     st_send, st_recv, gq_send, gq_recv, gf_send, gf_recv, qkv_send, qkv_recv, o_recv, o_all, wo_all,
+     proj_recv, f1_mine, f1_send, f1_recv, pair_recv, u_recv, out_recv,
      load_sem, big_sem, store_sem, send_sem, recv_sem) = refs
 
     row = lax.axis_index("row")
     col = lax.axis_index("col")
+    side = lax.rem(row, 2)
+    chip = row // 2
+    partner = chip * 2 + (1 - side)
+    across = lax.rem(row + 2, N_ROW)
 
     loads = {}
 
@@ -73,15 +79,17 @@
         for name, src, dst in (("wq", wq_in, wq), ("wk", wk_in, wk), ("wv", wv_in, wv)):
             if layer == 0:
                 small((name, layer), src.at[layer], dst.at[layer])
+    small(("wo", 1), wo_in.at[1], wo_all.at[col])
     for name, src, dst in (("b1", b1_in, b1), ("bq", bq_in, bq), ("bk", bk_in, bk), ("bv", bv_in, bv),
                            ("len", len_in, len_buf), ("bo", bo_in, bo), ("g2", g2_in, g2), ("b2", b2_in, b2),
                            ("bf1", bf1_in, bf1), ("bf2", bf2_in, bf2)):
         small(name, src, dst)
 
     barrier = pltpu.get_barrier_semaphore()
-    for off in range(1, 4):
-        pl.semaphore_signal(barrier, inc=1, device_id={"row": lax.rem(row + off, N_ROW)}, device_id_type=MESH)
-        pl.semaphore_signal(barrier, inc=1, device_id={"col": lax.rem(col + off, N_COL)}, device_id_type=MESH)
+    others = [{"col": lax.rem(col + a, N_COL), "row": lax.rem(row + b, N_ROW)}
+              for a in (2, 3, 1, 0) for b in (2, 3, 1, 0) if a or b]
+    for device in others:
+        pl.semaphore_signal(barrier, inc=1, device_id=device, device_id_type=MESH)
 
     def big(layer, stream, which):
         src, dst = (k_in, k_buf) if which == 0 else (v_in, v_buf)
@@ -94,7 +102,7 @@
             big(0, stream, which)
     for name, src, dst in (("wo", wo_in, wo), ("wf1", wf1_in, wf1), ("wf2", wf2_in, wf2)):
         small((name, 0), src.at[0], dst.at[0])
-    for name, src, dst in (("wq", wq_in, wq), ("wk", wk_in, wk), ("wv", wv_in, wv), ("wo", wo_in, wo),
+    for name, src, dst in (("wq", wq_in, wq), ("wk", wk_in, wk), ("wv", wv_in, wv),
                            ("wf1", wf1_in, wf1), ("wf2", wf2_in, wf2)):
         small((name, 1), src.at[1], dst.at[1])
     for stream in range(STREAMS):
@@ -108,31 +116,27 @@
             waited.add(name)
             loads[name].wait()
 
-    sends = []
+    drains = []
     recvs = {}
     n_sem = [0]
 
-    def exchange(tag, axis, src_of, dst_of):
+    def exchange(tag, copies, span):
+        index = n_sem[0]
+        n_sem[0] += 1
+        for src, dst, device in copies:
+            pltpu.make_async_remote_copy(
+                src_ref=src, dst_ref=dst, send_sem=send_sem.at[index],
+                recv_sem=recv_sem.at[index], device_id=device, device_id_type=MESH).start()
+        drains.append(pltpu.make_async_copy(span, span, send_sem.at[index]))
+        recvs[tag] = pltpu.make_async_copy(span, span, recv_sem.at[index])
+
+    def to_axis(tag, axis, src_of, buf):
         me = row if axis == "row" else col
-        waits = []
-        for off in (2, 3, 1):
-            dest = lax.rem(me + off, 4)
-            source = lax.rem(me + 4 - off, 4)
-            index = n_sem[0]
-            n_sem[0] += 1
-            out = pltpu.make_async_remote_copy(
-                src_ref=src_of(dest), dst_ref=dst_of(me), send_sem=send_sem.at[index],
-                recv_sem=recv_sem.at[index], device_id={axis: dest}, device_id_type=MESH)
-            out.start()
-            sends.append(out)
-            waits.append(pltpu.make_async_remote_copy(
-                src_ref=src_of(dest), dst_ref=dst_of(source), send_sem=send_sem.at[index],
-                recv_sem=recv_sem.at[index], device_id={axis: dest}, device_id_type=MESH))
-        recvs[tag] = waits
+        dests = [lax.rem(me + off, 4) for off in (2, 3, 1)]
+        exchange(tag, [(src_of(d), buf.at[me], {axis: d}) for d in dests], buf.at[0:3])
 
     def arrived(tag):
-        for copy in recvs[tag]:
-            copy.wait_recv()
+        recvs[tag].wait()
 
     def local_norm(state, gain):
         mean = jnp.sum(state, axis=-1, keepdims=True) * (1.0 / WIDTH)
@@ -145,21 +149,26 @@
             tile = jnp.concatenate([tile] * (128 // ROWS), axis=0)
         return normed, jnp.transpose(tile)[0:8]
 
-    def stat_columns(stats):
-        means = [stats[r, 0:1] for r in range(N_ROW)]
-        variances = [stats[r, 1:2] for r in range(N_ROW)]
-        mean = (means[0] + means[1] + means[2] + means[3]) * 0.25
-        gaps = [m - mean for m in means]
-        var = (variances[0] + variances[1] + variances[2] + variances[3]
-               + gaps[0] * gaps[0] + gaps[1] * gaps[1] + gaps[2] * gaps[2] + gaps[3] * gaps[3]) * 0.25
+    def merge_stats(blocks):
+        share = 1.0 / len(blocks)
+        mean = sum(m for m, _ in blocks) * share
+        var = sum(v + (m - mean) * (m - mean) for m, v in blocks) * share
+        return mean, var
+
+    def stat_columns(blocks):
+        mean, var = merge_stats(blocks)
         inv = lax.rsqrt(var + EPS_LN)
-        lines = [jnp.sqrt(v + EPS_LN) * inv for v in variances] + [g * inv for g in gaps]
+        lines = [jnp.sqrt(v + EPS_LN) * inv for _, v in blocks] + [(m - mean) * inv for m, _ in blocks]
         sub = lax.broadcasted_iota(jnp.int32, (8, 128), 0)
         tile = jnp.zeros((8, 128), F32)
         for i, line in enumerate(lines):
             tile = jnp.where(sub == i, line, tile)
         turned = jnp.transpose(jnp.concatenate([tile] * 16, axis=0))[0:ROWS]
-        return [turned[:, i:i + 1] for i in range(8)]
+        return [turned[:, i:i + 1] for i in range(len(lines))]
+
+    def block_stats(index, r):
+        tile = st_recv[index, r]
+        return tile[0:1], tile[1:2]
 
     def pack_heads(q, k, v, j, rows):
         half = rows // 2
@@ -193,18 +202,19 @@
             qkv_send[slot, j, ROWS:ROWS + HALF] = second.astype(BF16)
         qkv_recv[slot, row] = qkv_send[slot, row]
         if layer == 0 and stream == 0:
-            pl.semaphore_wait(barrier, 6)
-        exchange(("st1", slot), "row", lambda d: st_send.at[2 * slot], lambda s: st_recv.at[2 * slot, s])
-        exchange(("qkv", slot), "row", lambda d: qkv_send.at[slot, d], lambda s: qkv_recv.at[slot, s])
+            pl.semaphore_wait(barrier, N_PEER)
+        to_axis(("st1", slot), "row", lambda d: st_send.at[2 * slot], st_recv.at[2 * slot])
+        to_axis(("qkv", slot), "row", lambda d: qkv_send.at[slot, d], qkv_recv.at[slot])
+        if layer == 0 and stream == 0:
+            need(("wo", 1))
+            to_axis("wo", "col", lambda d: wo_all.at[col], wo_all)
 
     def affine_rows(gain, shift):
         sub = lax.broadcasted_iota(jnp.int32, (16, WIDTH), 0)
         return jnp.where(sub == 0, gain.astype(F32), jnp.where(sub == 1, shift.astype(F32), 0.0)).astype(BF16)
 
     def send_affine(layer, kind):
-        slot = layer * 2 + kind
         bias_on = jnp.where(row == 0, 1.0, 0.0)
-        sub = lax.broadcasted_iota(jnp.int32, (8, 128), 0)
         if kind == 0:
             for name in ("b1", "bq", "bk", "bv"):
                 need(name)
@@ -225,7 +235,9 @@
                 else:
                     first = jnp.where(low_half((8, 128)), swap_halves(qj), kj)
                     second = jnp.where(low_half((8, 128)), swap_halves(vj), vj)
-                gb_send[slot, j] = jnp.concatenate([first, second], axis=1)
+                gq_send[layer, j] = jnp.concatenate([first, second], axis=1)
+            gq_recv[layer, row] = gq_send[layer, row]
+            to_axis(("gb", layer, kind), "row", lambda d: gq_send.at[layer, d], gq_recv.at[layer])
         else:
             for name in ("g2", "b2", "bf1", ("wf1", layer)):
                 need(name)
@@ -233,29 +245,32 @@
             part = dot(rows, wf1[layer])[0:8]
             sub_w = lax.broadcasted_iota(jnp.int32, (8, FF_LOC), 0)
             part = part + jnp.where(sub_w == 1, bf1[layer:layer + 1, :].astype(F32) * bias_on, 0.0)
-            for j in range(N_ROW):
-                gb_send[slot, j] = part[:, j * WIDTH:(j + 1) * WIDTH]
-        gb_recv[slot, row] = gb_send[slot, row]
-        exchange(("gb", slot), "row", lambda d: gb_send.at[slot, d], lambda s: gb_recv.at[slot, s])
+            for j in range(2):
+                gf_send[layer, j] = part[:, j * FF_HALF:(j + 1) * FF_HALF]
+            gf_recv[layer, row] = gf_send[layer, side]
+            to_axis(("gb", layer, kind), "row", lambda d: gf_send.at[layer, lax.rem(d, 2)], gf_recv.at[layer])
 
     gb_done = set()
 
     def affine_lines(layer, kind):
-        slot = layer * 2 + kind
-        if slot not in gb_done:
-            gb_done.add(slot)
-            arrived(("gb", slot))
-        tiles = [gb_recv[slot, r] for r in range(N_ROW)]
-        gains = [t[0:1] for t in tiles]
-        const = tiles[0][1:2] + tiles[1][1:2] + tiles[2][1:2] + tiles[3][1:2]
-        return gains, const
+        if (layer, kind) not in gb_done:
+            gb_done.add((layer, kind))
+            arrived(("gb", layer, kind))
+
+    def gain_line(buf, layer, r):
+        return buf[layer, r, 0:1]
+
+    def const_line(buf, layer):
+        return buf[layer, 0, 1:2] + buf[layer, 1, 1:2] + buf[layer, 2, 1:2] + buf[layer, 3, 1:2]
 
     def attend(layer, stream):
         slot = layer * STREAMS + stream
         span = slice(stream * ROWS, (stream + 1) * ROWS)
         arrived(("st1", slot))
-        cols = stat_columns(st_recv[2 * slot])
-        gains, const = affine_lines(layer, 0)
+        cols = stat_columns([block_stats(2 * slot, r) for r in range(N_ROW)])
+        affine_lines(layer, 0)
+        gains = [gain_line(gq_recv, layer, r) for r in range(N_ROW)]
+        const = const_line(gq_recv, layer)
         arrived(("qkv", slot))
         low = low_half((HALF, 128))
         qk = const[:, 0:128]
@@ -305,29 +320,41 @@
                 acc = acc + jnp.where(q_row == 2 * j + q_half, wide[:, j * 128:(j + 1) * 128], 0.0)
             o_mix[g * GROUP:(g + 1) * GROUP, :] = acc + swap_halves(acc)
         o2 = o_mix[...] + prob_new * v2.astype(F32)
-        o_recv[slot, row] = jnp.where(low, o2[0:HALF], o2[HALF:ROWS]).astype(BF16)
-        exchange(("o", slot), "row", lambda d: o_recv.at[slot, row], lambda s: o_recv.at[slot, s])
-
-    def project(layer, stream):
-        slot = layer * STREAMS + stream
-        need(("wo", layer))
-        arrived(("o", slot))
+        packed = jnp.where(low, o2[0:HALF], o2[HALF:ROWS]).astype(BF16)
+        if layer == 0:
+            o_recv[stream, row] = packed
+            to_axis(("o", slot), "row", lambda d: o_recv.at[stream, row], o_recv.at[stream])
+        else:
+            head = col * N_ROW + row
+            o_all[stream, head] = packed
+            mine = o_all.at[stream, head]
+            exchange(("o", slot), [(mine, mine, d) for d in others], o_all.at[stream, 0:N_PEER])
+
+    def unpack_heads(buf, first):
         low = low_half((HALF, 128))
-        parts = [o_recv[slot, r].astype(F32) for r in range(N_ROW)]
+        parts = [buf[first + r].astype(F32) for r in range(N_ROW)]
         turns = [swap_halves(p) for p in parts]
         pairs = []
         for a, b in ((0, 1), (2, 3)):
             top = jnp.where(low, parts[a], turns[b])
             bottom = jnp.where(low, turns[a], parts[b])
             pairs.append(jnp.concatenate([top, bottom], axis=0).astype(BF16))
-        proj_recv[slot, col] = dot(jnp.concatenate(pairs, axis=1), wo[layer]).astype(BF16)
-        exchange(("proj", slot), "col", lambda d: proj_recv.at[slot, col], lambda s: proj_recv.at[slot, s])
-
-    def residual(slot, buf, bias, stream):
+        return jnp.concatenate(pairs, axis=1)
+
+    def project(stream):
+        need(("wo", 0))
+        arrived(("o", stream))
+        proj_recv[stream, col] = dot(unpack_heads(o_recv.at[stream], 0), wo[0]).astype(BF16)
+        to_axis(("proj", stream), "col", lambda d: proj_recv.at[stream, col], proj_recv.at[stream])
+
+    def col_sum(buf):
+        total = buf[0].astype(F32)
+        for c in range(1, N_COL):
+            total = total + buf[c].astype(F32)
+        return total
+
+    def residual(total, bias, stream):
         span = slice(stream * ROWS, (stream + 1) * ROWS)
-        total = buf[slot, 0].astype(F32)
-        for c in range(1, N_COL):
-            total = total + buf[slot, c].astype(F32)
         new = (x_buf[span, :].astype(F32) + (total + bias)).astype(BF16)
         x_buf[span, :] = new
         return new.astype(F32)
@@ -337,44 +364,71 @@
         need("bo")
         need("g2")
         need(("wf1", layer))
-        arrived(("proj", slot))
-        state = residual(slot, proj_recv, bo[layer:layer + 1, :].astype(F32), stream)
+        if layer == 0:
+            arrived(("proj", stream))
+            total = col_sum(proj_recv.at[stream])
+        else:
+            if "wo" in recvs:
+                recvs.pop("wo").wait()
+            arrived(("o", slot))
+            total = dot(unpack_heads(o_all.at[stream], 0), wo_all[0])
+            for c in range(1, N_COL):
+                total = total + dot(unpack_heads(o_all.at[stream], c * N_ROW), wo_all[c])
+        state = residual(total, bo[layer:layer + 1, :].astype(F32), stream)
         normed, tile = local_norm(state, g2[layer:layer + 1, :].astype(F32))
-        st_send[2 * slot + 1] = tile
-        st_recv[2 * slot + 1, row] = tile
-        exchange(("st2", slot), "row", lambda d: st_send.at[2 * slot + 1], lambda s: st_recv.at[2 * slot + 1, s])
-        for j in range(N_ROW):
-            f1_send[slot, j] = dot(normed, wf1[layer, :, j * WIDTH:(j + 1) * WIDTH]).astype(BF16)
-        f1_recv[slot, row] = f1_send[slot, row]
-        exchange(("f1", slot), "row", lambda d: f1_send.at[slot, d], lambda s: f1_recv.at[slot, s])
+        index = 2 * slot + 1
+        st_send[index] = tile
+        st_recv[index, row] = tile
+        mine = st_send.at[index]
+        spot = st_recv.at[index, row]
+        exchange(("st2", slot), [(mine, spot, {"row": partner})], mine)
+        far = lax.rem(partner + 2, N_ROW)
+        exchange(("st3", slot), [(mine, spot, {"row": across}), (mine, spot, {"row": far})], st_recv.at[index, 0:2])
+        theirs = pl.ds(pl.multiple_of((1 - side) * FF_HALF, FF_HALF), FF_HALF)
+        f1_send[slot] = dot(normed, wf1[layer, :, theirs]).astype(BF16)
+        exchange(("f1", slot), [(f1_send.at[slot], f1_recv.at[slot], {"row": partner})], f1_recv.at[slot])
+        ours = pl.ds(pl.multiple_of(side * FF_HALF, FF_HALF), FF_HALF)
+        f1_mine[stream] = dot(normed, wf1[layer, :, ours])
+
+    def send_pair(layer, stream):
+        slot = layer * STREAMS + stream
+        arrived(("st2", slot))
+        cols = stat_columns([block_stats(2 * slot + 1, r) for r in (row, partner)])
+        affine_lines(layer, 1)
+        arrived(("f1", slot))
+        total = f1_mine[stream] * cols[0] + cols[2] * gain_line(gf_recv, layer, row)
+        total = total + f1_recv[slot].astype(F32) * cols[1] + cols[3] * gain_line(gf_recv, layer, partner)
+        pair_recv[slot, chip] = total.astype(BF16)
+        mine = pair_recv.at[slot, chip]
+        exchange(("pair", slot), [(mine, mine, {"row": across})], mine)
 
     def send_act(layer, stream):
         slot = layer * STREAMS + stream
-        arrived(("st2", slot))
-        cols = stat_columns(st_recv[2 * slot + 1])
-        gains, const = affine_lines(layer, 1)
-        arrived(("f1", slot))
-        total = const
-        for r in range(N_ROW):
-            total = total + f1_recv[slot, r].astype(F32) * cols[r] + cols[4 + r] * gains[r]
-        u_recv[slot, row] = jnp.maximum(total, 0.0).astype(BF16)
-        exchange(("u", slot), "row", lambda d: u_recv.at[slot, row], lambda s: u_recv.at[slot, s])
+        arrived(("st3", slot))
+        pairs = [merge_stats([block_stats(2 * slot + 1, 2 * k + r) for r in range(2)]) for k in range(2)]
+        cols = stat_columns(pairs)
+        total = const_line(gf_recv, layer)
+        arrived(("pair", slot))
+        for k in range(2):
+            gain = gain_line(gf_recv, layer, 2 * k) + gain_line(gf_recv, layer, 2 * k + 1)
+            total = total + pair_recv[slot, k].astype(F32) * cols[k] + cols[2 + k] * gain
+        u_recv[slot, side] = jnp.maximum(total, 0.0).astype(BF16)
+        mine = u_recv.at[slot, side]
+        exchange(("u", slot), [(mine, mine, {"row": partner})], mine)
 
     def send_out(layer, stream):
         slot = layer * STREAMS + stream
         need(("wf2", layer))
         arrived(("u", slot))
-        acc = dot(u_recv[slot, 0], wf2[layer, 0:WIDTH, :])
-        for r in range(1, N_ROW):
-            acc = acc + dot(u_recv[slot, r], wf2[layer, r * WIDTH:(r + 1) * WIDTH, :])
+        acc = dot(u_recv[slot, 0], wf2[layer, 0:FF_HALF, :]) + dot(u_recv[slot, 1], wf2[layer, FF_HALF:, :])
         out_recv[slot, col] = acc.astype(BF16)
-        exchange(("out", slot), "col", lambda d: out_recv.at[slot, col], lambda s: out_recv.at[slot, s])
+        to_axis(("out", slot), "col", lambda d: out_recv.at[slot, col], out_recv.at[slot])
 
     def finish(layer, stream):
         slot = layer * STREAMS + stream
         need("bf2")
         arrived(("out", slot))
-        residual(slot, out_recv, bf2[layer:layer + 1, :].astype(F32), stream)
+        residual(col_sum(out_recv.at[slot]), bf2[layer:layer + 1, :].astype(F32), stream)
 
     stores = []
 
@@ -396,15 +450,17 @@
         store(kv_turn.at[layer, HEAD:2 * HEAD], v_out.at[layer], 2 * layer + 1)
         if layer == 0:
             send_affine(0, 1)
-        for stream in range(STREAMS):
-            project(layer, stream)
         if layer == 0:
+            for stream in range(STREAMS):
+                project(stream)
             for name in MAT_NAMES[:3]:
                 need((name, 1))
             send_affine(1, 0)
             send_affine(1, 1)
         for stream in range(STREAMS):
             send_inner(layer, stream)
+        for stream in range(STREAMS):
+            send_pair(layer, stream)
         for stream in range(STREAMS):
             send_act(layer, stream)
         for stream in range(STREAMS):
@@ -418,20 +474,27 @@
                 store(x_buf.at[span], h_out.at[span], 2 * LAYERS + stream)
     for copy in stores:
         copy.wait()
-    for copy in sends:
-        copy.wait_send()
+    for copy in drains:
+        copy.wait()
 
 
 N_SLOT = LAYERS * STREAMS
-N_COPY = 3 * (8 * N_SLOT - 0 + 2 * LAYERS)
-
-
-def emit_kernel(h_in, k_in, v_in, h_out, k_out, v_out, sem):
-    copies = [pltpu.make_async_copy(src, dst, sem.at[i])
-              for i, (src, dst) in enumerate(((h_in, h_out), (k_in, k_out), (v_in, v_out)))]
-    for copy in copies:
+N_COPY = 9 * N_SLOT + STREAMS + 2 * LAYERS + 1
+N_PEER = N_ROW * N_COL - 1
+
+
+def emit_kernel(h_in, k_in, v_in, h_out, k_out, v_out, h_buf, k_buf, v_buf, sem):
+    moves = ((h_in, h_buf, h_out), (k_in, k_buf, k_out), (v_in, v_buf, v_out))
+    loads = [pltpu.make_async_copy(src, buf, sem.at[i]) for i, (src, buf, _) in enumerate(moves)]
+    for copy in loads:
         copy.start()
-    for copy in copies:
+    stores = []
+    for i, (_, buf, dst) in enumerate(moves):
+        loads[i].wait()
+        copy = pltpu.make_async_copy(buf, dst, sem.at[i])
+        copy.start()
+        stores.append(copy)
+    for copy in stores:
         copy.wait()
 
 
@@ -452,15 +515,21 @@
         vm((ROWS, 128), F32),
         vm((2 * N_SLOT, 8, 128), F32),
         vm((2 * N_SLOT, N_ROW, 8, 128), F32),
-        vm((2 * LAYERS, N_ROW, 8, WIDTH), F32),
-        vm((2 * LAYERS, N_ROW, 8, WIDTH), F32),
+        vm((LAYERS, N_ROW, 8, WIDTH), F32),
+        vm((LAYERS, N_ROW, 8, WIDTH), F32),
+        vm((LAYERS, 2, 8, FF_HALF), F32),
+        vm((LAYERS, N_ROW, 8, FF_HALF), F32),
         vm((N_SLOT, N_ROW, ROWS + HALF, 128), BF16),
         vm((N_SLOT, N_ROW, ROWS + HALF, 128), BF16),
-        vm((N_SLOT, N_ROW, HALF, 128), BF16),
-        vm((N_SLOT, N_COL, ROWS, WIDTH), BF16),
-        vm((N_SLOT, N_ROW, ROWS, WIDTH), BF16),
-        vm((N_SLOT, N_ROW, ROWS, WIDTH), BF16),
-        vm((N_SLOT, N_ROW, ROWS, WIDTH), BF16),
+        vm((STREAMS, N_ROW, HALF, 128), BF16),
+        vm((STREAMS, N_ROW * N_COL, HALF, 128), BF16),
+        vm((N_COL, WIDTH, WIDTH), BF16),
+        vm((STREAMS, N_COL, ROWS, WIDTH), BF16),
+        vm((STREAMS, ROWS, FF_HALF), F32),
+        vm((N_SLOT, ROWS, FF_HALF), BF16),
+        vm((N_SLOT, ROWS, FF_HALF), BF16),
+        vm((N_SLOT, 2, ROWS, FF_HALF), BF16),
+        vm((N_SLOT, 2, ROWS, FF_HALF), BF16),
         vm((N_SLOT, N_COL, ROWS, WIDTH), BF16),
         pltpu.SemaphoreType.DMA((32,)),
         pltpu.SemaphoreType.DMA((2 * N_SLOT,)),
@@ -484,10 +553,10 @@
     h_out, k_new, v_new = pl.pallas_call(
         emit_kernel,
         out_shape=shapes,
-        in_specs=[pl.BlockSpec(memory_space=pltpu.VMEM)] * 3,
+        in_specs=[any_spec] * 3,
         out_specs=(pl.BlockSpec(memory_space=pltpu.HBM),) * 3,
-        scratch_shapes=[pltpu.SemaphoreType.DMA((3,))],
-        compiler_params=pltpu.CompilerParams(vmem_limit_bytes=1024 * 1024),
+        scratch_shapes=[vm(a.shape, a.dtype) for a in shapes] + [pltpu.SemaphoreType.DMA((3,))],
+        compiler_params=pltpu.CompilerParams(vmem_limit_bytes=60 * 1024 * 1024),
         name="emit",
     )(*results)
 

time: 71.9 us -> 68.7 us (0.955)
  local copies, waits for them, and re-layouts: 2.35 us -> 0 us
    unnamed x6 -> x0, local copies, waits for them, and re-layouts: 2.35 us -> none
    pallas_call x1, Pallas kernels: 67.9 us -> 66.4 us  [run_step(): pl.pallas_call(step_kernel, out_shape=shapes, in_specs=[pl.BlockSpec(memo...]
    pallas_call x1, Pallas kernels: 0.67 us -> 1.51 us  [run_step(): pl.pallas_call(emit_kernel, out_shape=shapes, in_specs=[any_spec] * 3, ou...]
where the time goes in v3:
time: 68.7 us; the launch traced here: 68.5 us
  Pallas kernels  67.9 us (99%)
    pallas_call x1, Pallas kernels, run_step(): pl.pallas_call(step_kernel, out_shape=shapes, in_specs=[pl.BlockSpec(memo...  66.4 us
    pallas_call x1, Pallas kernels, run_step(): pl.pallas_call(emit_kernel, out_shape=shapes, in_specs=[any_spec] * 3, ou...  1.51 us

profile of v3, /device:TPU:0, one launch (start us, length us, event | category | flops | bytes accessed | tf_op | source)
XLA Modules:
  0.0 68.5 jit_solution(17826922351859061246)
XLA Ops:
  0.6 66.4 %decode_step.1 = (bf16[128,256]{1,0:T(8,128)(2,1)}, bf16[2,64,128]{2,1,0:T(8,128)(2,1)}, bf16[2,64,128]{2,1,0:T(8,128)(2,1)}) custom-call(bf16[128,256]{1,0:T(8,128)(2,1)} %refs_0_.1, s32[1,128]{1,0:T(1,128)} %bitcast.19, bf16[2,8192,512]{2,1,0:T(8,128)(2,1)} %bitcast.17, bf16[2,8192,512]{2,1,0:T(8,128)(2,1)} %bitcast.18, bf16[2,256]{1,0:T(2,128)(2,1)} %refs_4_.1, ...), custom_call_target="tpu_custom_call" | custom-call | tf_op jit(solution)/shard_map/decode_step/pallas_call | solution.py:543
  67.0 1.5 %emit.1 = (bf16[128,256]{1,0:T(8,128)(2,1)}, bf16[2,64,128]{2,1,0:T(8,128)(2,1)}, bf16[2,64,128]{2,1,0:T(8,128)(2,1)}) custom-call(bf16[128,256]{1,0:T(8,128)(2,1)} %get-tuple-element.9.h_in, bf16[2,64,128]{2,1,0:T(8,128)(2,1)} %get-tuple-element.10.k_in, bf16[2,64,128]{2,1,0:T(8,128)(2,1)} %get-tuple-element.11.v_in), custom_call_target="tpu_custom_call" | custom-call | tf_op jit(solution)/shard_map/emit/pallas_call | solution.py:553

commit v4 on v3

--- a/solution.py
+++ b/solution.py
@@ -205,9 +205,6 @@
             pl.semaphore_wait(barrier, N_PEER)
         to_axis(("st1", slot), "row", lambda d: st_send.at[2 * slot], st_recv.at[2 * slot])
         to_axis(("qkv", slot), "row", lambda d: qkv_send.at[slot, d], qkv_recv.at[slot])
-        if layer == 0 and stream == 0:
-            need(("wo", 1))
-            to_axis("wo", "col", lambda d: wo_all.at[col], wo_all)
 
     def affine_rows(gain, shift):
         sub = lax.broadcasted_iota(jnp.int32, (16, WIDTH), 0)
@@ -459,6 +456,9 @@
             send_affine(1, 1)
         for stream in range(STREAMS):
             send_inner(layer, stream)
+        if layer == 0:
+            need(("wo", 1))
+            to_axis("wo", "col", lambda d: wo_all.at[col], wo_all)
         for stream in range(STREAMS):
             send_pair(layer, stream)
         for stream in range(STREAMS):

time: 68.7 us -> 74.5 us (1.084)
  Pallas kernels: 67.9 us -> 73.7 us
    pallas_call x1, Pallas kernels: 66.4 us -> 72.2 us  [run_step(): pl.pallas_call(step_kernel, out_shape=shapes, in_specs=[pl.BlockSpec(memo...]
where the time goes in v4:
time: 74.5 us; the launch traced here: 74.3 us
  Pallas kernels  73.7 us (99%)
    pallas_call x1, Pallas kernels, run_step(): pl.pallas_call(step_kernel, out_shape=shapes, in_specs=[pl.BlockSpec(memo...  72.2 us
    pallas_call x1, Pallas kernels, run_step(): pl.pallas_call(emit_kernel, out_shape=shapes, in_specs=[any_spec] * 3, ou...  1.51 us

profile of v4, /device:TPU:0, one launch (start us, length us, event | category | flops | bytes accessed | tf_op | source)
XLA Modules:
  0.0 74.3 jit_solution(7618530334468520122)
XLA Ops:
  0.6 72.2 %decode_step.1 = (bf16[128,256]{1,0:T(8,128)(2,1)}, bf16[2,64,128]{2,1,0:T(8,128)(2,1)}, bf16[2,64,128]{2,1,0:T(8,128)(2,1)}) custom-call(bf16[128,256]{1,0:T(8,128)(2,1)} %refs_0_.1, s32[1,128]{1,0:T(1,128)} %bitcast.19, bf16[2,8192,512]{2,1,0:T(8,128)(2,1)} %bitcast.17, bf16[2,8192,512]{2,1,0:T(8,128)(2,1)} %bitcast.18, bf16[2,256]{1,0:T(2,128)(2,1)} %refs_4_.1, ...), custom_call_target="tpu_custom_call" | custom-call | tf_op jit(solution)/shard_map/decode_step/pallas_call | solution.py:543
  72.8 1.5 %emit.1 = (bf16[128,256]{1,0:T(8,128)(2,1)}, bf16[2,64,128]{2,1,0:T(8,128)(2,1)}, bf16[2,64,128]{2,1,0:T(8,128)(2,1)}) custom-call(bf16[128,256]{1,0:T(8,128)(2,1)} %get-tuple-element.9.h_in, bf16[2,64,128]{2,1,0:T(8,128)(2,1)} %get-tuple-element.10.k_in, bf16[2,64,128]{2,1,0:T(8,128)(2,1)} %get-tuple-element.11.v_in), custom_call_target="tpu_custom_call" | custom-call | tf_op jit(solution)/shard_map/emit/pallas_call | solution.py:553

commit v5 on v4

--- a/solution.py
+++ b/solution.py
@@ -49,7 +49,7 @@
      h_out, k_out, v_out,
      x_buf, len_buf, k_buf, v_buf, g1, b1, wq, bq, wk, bk, wv, bv, wo, bo, g2, b2, wf1, bf1, wf2, bf2,
      len_mat, kv_mix, kv_turn, s_buf, p_buf, o_mix,
-     st_send, st_recv, gq_send, gq_recv, gf_send, gf_recv, qkv_send, qkv_recv, o_recv, o_all, wo_all,
+     st_send, st_recv, gq_send, gq_recv, gf_send, gf_recv, qkv_send, qkv_recv, o_recv,
      proj_recv, f1_mine, f1_send, f1_recv, pair_recv, u_recv, out_recv,
      load_sem, big_sem, store_sem, send_sem, recv_sem) = refs
 
@@ -79,17 +79,15 @@
         for name, src, dst in (("wq", wq_in, wq), ("wk", wk_in, wk), ("wv", wv_in, wv)):
             if layer == 0:
                 small((name, layer), src.at[layer], dst.at[layer])
-    small(("wo", 1), wo_in.at[1], wo_all.at[col])
     for name, src, dst in (("b1", b1_in, b1), ("bq", bq_in, bq), ("bk", bk_in, bk), ("bv", bv_in, bv),
                            ("len", len_in, len_buf), ("bo", bo_in, bo), ("g2", g2_in, g2), ("b2", b2_in, b2),
                            ("bf1", bf1_in, bf1), ("bf2", bf2_in, bf2)):
         small(name, src, dst)
 
     barrier = pltpu.get_barrier_semaphore()
-    others = [{"col": lax.rem(col + a, N_COL), "row": lax.rem(row + b, N_ROW)}
-              for a in (2, 3, 1, 0) for b in (2, 3, 1, 0) if a or b]
-    for device in others:
-        pl.semaphore_signal(barrier, inc=1, device_id=device, device_id_type=MESH)
+    for off in range(1, 4):
+        pl.semaphore_signal(barrier, inc=1, device_id={"row": lax.rem(row + off, N_ROW)}, device_id_type=MESH)
+        pl.semaphore_signal(barrier, inc=1, device_id={"col": lax.rem(col + off, N_COL)}, device_id_type=MESH)
 
     def big(layer, stream, which):
         src, dst = (k_in, k_buf) if which == 0 else (v_in, v_buf)
@@ -102,7 +100,7 @@
             big(0, stream, which)
     for name, src, dst in (("wo", wo_in, wo), ("wf1", wf1_in, wf1), ("wf2", wf2_in, wf2)):
         small((name, 0), src.at[0], dst.at[0])
-    for name, src, dst in (("wq", wq_in, wq), ("wk", wk_in, wk), ("wv", wv_in, wv),
+    for name, src, dst in (("wq", wq_in, wq), ("wk", wk_in, wk), ("wv", wv_in, wv), ("wo", wo_in, wo),
                            ("wf1", wf1_in, wf1), ("wf2", wf2_in, wf2)):
         small((name, 1), src.at[1], dst.at[1])
     for stream in range(STREAMS):
@@ -318,14 +316,8 @@
             o_mix[g * GROUP:(g + 1) * GROUP, :] = acc + swap_halves(acc)
         o2 = o_mix[...] + prob_new * v2.astype(F32)
         packed = jnp.where(low, o2[0:HALF], o2[HALF:ROWS]).astype(BF16)
-        if layer == 0:
-            o_recv[stream, row] = packed
-            to_axis(("o", slot), "row", lambda d: o_recv.at[stream, row], o_recv.at[stream])
-        else:
-            head = col * N_ROW + row
-            o_all[stream, head] = packed
-            mine = o_all.at[stream, head]
-            exchange(("o", slot), [(mine, mine, d) for d in others], o_all.at[stream, 0:N_PEER])
+        o_recv[slot, row] = packed
+        to_axis(("o", slot), "row", lambda d: o_recv.at[slot, row], o_recv.at[slot])
 
     def unpack_heads(buf, first):
         low = low_half((HALF, 128))
@@ -338,11 +330,12 @@
             pairs.append(jnp.concatenate([top, bottom], axis=0).astype(BF16))
         return jnp.concatenate(pairs, axis=1)
 
-    def project(stream):
-        need(("wo", 0))
-        arrived(("o", stream))
-        proj_recv[stream, col] = dot(unpack_heads(o_recv.at[stream], 0), wo[0]).astype(BF16)
-        to_axis(("proj", stream), "col", lambda d: proj_recv.at[stream, col], proj_recv.at[stream])
+    def project(layer, stream):
+        slot = layer * STREAMS + stream
+        need(("wo", layer))
+        arrived(("o", slot))
+        proj_recv[slot, col] = dot(unpack_heads(o_recv.at[slot], 0), wo[layer]).astype(BF16)
+        to_axis(("proj", slot), "col", lambda d: proj_recv.at[slot, col], proj_recv.at[slot])
 
     def col_sum(buf):
         total = buf[0].astype(F32)
@@ -361,16 +354,8 @@
         need("bo")
         need("g2")
         need(("wf1", layer))
-        if layer == 0:
-            arrived(("proj", stream))
-            total = col_sum(proj_recv.at[stream])
-        else:
-            if "wo" in recvs:
-                recvs.pop("wo").wait()
-            arrived(("o", slot))
-            total = dot(unpack_heads(o_all.at[stream], 0), wo_all[0])
-            for c in range(1, N_COL):
-                total = total + dot(unpack_heads(o_all.at[stream], c * N_ROW), wo_all[c])
+        arrived(("proj", slot))
+        total = col_sum(proj_recv.at[slot])
         state = residual(total, bo[layer:layer + 1, :].astype(F32), stream)
         normed, tile = local_norm(state, g2[layer:layer + 1, :].astype(F32))
         index = 2 * slot + 1
@@ -447,18 +432,15 @@
         store(kv_turn.at[layer, HEAD:2 * HEAD], v_out.at[layer], 2 * layer + 1)
         if layer == 0:
             send_affine(0, 1)
+        for stream in range(STREAMS):
+            project(layer, stream)
         if layer == 0:
-            for stream in range(STREAMS):
-                project(stream)
             for name in MAT_NAMES[:3]:
                 need((name, 1))
             send_affine(1, 0)
             send_affine(1, 1)
         for stream in range(STREAMS):
             send_inner(layer, stream)
-        if layer == 0:
-            need(("wo", 1))
-            to_axis("wo", "col", lambda d: wo_all.at[col], wo_all)
         for stream in range(STREAMS):
             send_pair(layer, stream)
         for stream in range(STREAMS):
@@ -479,8 +461,8 @@
 
 
 N_SLOT = LAYERS * STREAMS
-N_COPY = 9 * N_SLOT + STREAMS + 2 * LAYERS + 1
-N_PEER = N_ROW * N_COL - 1
+N_COPY = 10 * N_SLOT + 2 * LAYERS
+N_PEER = N_ROW + N_COL - 2
 
 
 def emit_kernel(h_in, k_in, v_in, h_out, k_out, v_out, h_buf, k_buf, v_buf, sem):
@@ -521,10 +503,8 @@
         vm((LAYERS, N_ROW, 8, FF_HALF), F32),
         vm((N_SLOT, N_ROW, ROWS + HALF, 128), BF16),
         vm((N_SLOT, N_ROW, ROWS + HALF, 128), BF16),
-        vm((STREAMS, N_ROW, HALF, 128), BF16),
-        vm((STREAMS, N_ROW * N_COL, HALF, 128), BF16),
-        vm((N_COL, WIDTH, WIDTH), BF16),
-        vm((STREAMS, N_COL, ROWS, WIDTH), BF16),
+        vm((N_SLOT, N_ROW, HALF, 128), BF16),
+        vm((N_SLOT, N_COL, ROWS, WIDTH), BF16),
         vm((STREAMS, ROWS, FF_HALF), F32),
         vm((N_SLOT, ROWS, FF_HALF), BF16),
         vm((N_SLOT, ROWS, FF_HALF), BF16),

time: 74.5 us -> 68.9 us (0.925)
  Pallas kernels: 73.7 us -> 68.1 us
    pallas_call x1, Pallas kernels: 72.2 us -> 66.6 us  [run_step(): pl.pallas_call(step_kernel, out_shape=shapes, in_specs=[pl.BlockSpec(memo...]
where the time goes in v5:
time: 68.9 us; the launch traced here: 68.8 us
  Pallas kernels  68.1 us (99%)
    pallas_call x1, Pallas kernels, run_step(): pl.pallas_call(step_kernel, out_shape=shapes, in_specs=[pl.BlockSpec(memo...  66.6 us
    pallas_call x1, Pallas kernels, run_step(): pl.pallas_call(emit_kernel, out_shape=shapes, in_specs=[any_spec] * 3, ou...  1.51 us

profile of v5, /device:TPU:0, one launch (start us, length us, event | category | flops | bytes accessed | tf_op | source)
XLA Modules:
  0.0 68.8 jit_solution(14365823779809916693)
XLA Ops:
  0.6 66.6 %decode_step.1 = (bf16[128,256]{1,0:T(8,128)(2,1)}, bf16[2,64,128]{2,1,0:T(8,128)(2,1)}, bf16[2,64,128]{2,1,0:T(8,128)(2,1)}) custom-call(bf16[128,256]{1,0:T(8,128)(2,1)} %refs_0_.1, s32[1,128]{1,0:T(1,128)} %bitcast.19, bf16[2,8192,512]{2,1,0:T(8,128)(2,1)} %bitcast.17, bf16[2,8192,512]{2,1,0:T(8,128)(2,1)} %bitcast.18, bf16[2,256]{1,0:T(2,128)(2,1)} %refs_4_.1, ...), custom_call_target="tpu_custom_call" | custom-call | tf_op jit(solution)/shard_map/decode_step/pallas_call | solution.py:523
  67.3 1.5 %emit.1 = (bf16[128,256]{1,0:T(8,128)(2,1)}, bf16[2,64,128]{2,1,0:T(8,128)(2,1)}, bf16[2,64,128]{2,1,0:T(8,128)(2,1)}) custom-call(bf16[128,256]{1,0:T(8,128)(2,1)} %get-tuple-element.9.h_in, bf16[2,64,128]{2,1,0:T(8,128)(2,1)} %get-tuple-element.10.k_in, bf16[2,64,128]{2,1,0:T(8,128)(2,1)} %get-tuple-element.11.v_in), custom_call_target="tpu_custom_call" | custom-call | tf_op jit(solution)/shard_map/emit/pallas_call | solution.py:533

commit v6 on v5

--- a/solution.py
+++ b/solution.py
@@ -14,7 +14,7 @@
 
 LAYERS = 2
 BATCH = 128
-STREAMS = 2
+STREAMS = 4
 ROWS = BATCH // STREAMS
 HALF = ROWS // 2
 GROUP = 16

time: 68.9 us -> 71 us (1.030)
  Pallas kernels: 68.1 us -> 70.2 us
    pallas_call x1, Pallas kernels: 66.6 us -> 68.7 us  [run_step(): pl.pallas_call(step_kernel, out_shape=shapes, in_specs=[pl.BlockSpec(memo...]
where the time goes in v6:
time: 71 us; the launch traced here: 70.8 us
  Pallas kernels  70.2 us (99%)
    pallas_call x1, Pallas kernels, run_step(): pl.pallas_call(step_kernel, out_shape=shapes, in_specs=[pl.BlockSpec(memo...  68.7 us
    pallas_call x1, Pallas kernels, run_step(): pl.pallas_call(emit_kernel, out_shape=shapes, in_specs=[any_spec] * 3, ou...  1.51 us

profile of v6, /device:TPU:0, one launch (start us, length us, event | category | flops | bytes accessed | tf_op | source)
XLA Modules:
  0.0 70.8 jit_solution(6377716447590079474)
XLA Ops:
  0.6 68.7 %decode_step.1 = (bf16[128,256]{1,0:T(8,128)(2,1)}, bf16[2,64,128]{2,1,0:T(8,128)(2,1)}, bf16[2,64,128]{2,1,0:T(8,128)(2,1)}) custom-call(bf16[128,256]{1,0:T(8,128)(2,1)} %refs_0_.1, s32[1,128]{1,0:T(1,128)} %bitcast.19, bf16[2,8192,512]{2,1,0:T(8,128)(2,1)} %bitcast.17, bf16[2,8192,512]{2,1,0:T(8,128)(2,1)} %bitcast.18, bf16[2,256]{1,0:T(2,128)(2,1)} %refs_4_.1, ...), custom_call_target="tpu_custom_call" | custom-call | tf_op jit(solution)/shard_map/decode_step/pallas_call | solution.py:523
  69.3 1.5 %emit.1 = (bf16[128,256]{1,0:T(8,128)(2,1)}, bf16[2,64,128]{2,1,0:T(8,128)(2,1)}, bf16[2,64,128]{2,1,0:T(8,128)(2,1)}) custom-call(bf16[128,256]{1,0:T(8,128)(2,1)} %get-tuple-element.9.h_in, bf16[2,64,128]{2,1,0:T(8,128)(2,1)} %get-tuple-element.10.k_in, bf16[2,64,128]{2,1,0:T(8,128)(2,1)} %get-tuple-element.11.v_in), custom_call_target="tpu_custom_call" | custom-call | tf_op jit(solution)/shard_map/emit/pallas_call | solution.py:533

commit v7 on v5

--- a/solution.py
+++ b/solution.py
@@ -18,6 +18,7 @@
 ROWS = BATCH // STREAMS
 HALF = ROWS // 2
 GROUP = 16
+COL_PIECES = 4
 N_ROW = 4
 N_COL = 4
 HEAD = 64
@@ -127,6 +128,15 @@
                 recv_sem=recv_sem.at[index], device_id=device, device_id_type=MESH).start()
         drains.append(pltpu.make_async_copy(span, span, send_sem.at[index]))
         recvs[tag] = pltpu.make_async_copy(span, span, recv_sem.at[index])
+
+    def to_col(tag, buf):
+        peers = (3 - col, lax.rem(col + 2, N_COL), col + 1 - 2 * lax.rem(col, 2))
+        rows = ROWS // COL_PIECES
+        copies = []
+        for piece in range(COL_PIECES):
+            mine = buf.at[col, piece * rows:(piece + 1) * rows]
+            copies += [(mine, mine, {"col": peer}) for peer in peers]
+        exchange(tag, copies, buf.at[0:3])
 
     def to_axis(tag, axis, src_of, buf):
         me = row if axis == "row" else col
@@ -335,7 +345,7 @@
         need(("wo", layer))
         arrived(("o", slot))
         proj_recv[slot, col] = dot(unpack_heads(o_recv.at[slot], 0), wo[layer]).astype(BF16)
-        to_axis(("proj", slot), "col", lambda d: proj_recv.at[slot, col], proj_recv.at[slot])
+        to_col(("proj", slot), proj_recv.at[slot])
 
     def col_sum(buf):
         total = buf[0].astype(F32)
@@ -404,7 +414,7 @@
         arrived(("u", slot))
         acc = dot(u_recv[slot, 0], wf2[layer, 0:FF_HALF, :]) + dot(u_recv[slot, 1], wf2[layer, FF_HALF:, :])
         out_recv[slot, col] = acc.astype(BF16)
-        to_axis(("out", slot), "col", lambda d: out_recv.at[slot, col], out_recv.at[slot])
+        to_col(("out", slot), out_recv.at[slot])
 
     def finish(layer, stream):
         slot = layer * STREAMS + stream

time: 68.9 us -> 68.4 us (level)
  no operation moved by 1% of the time
where the time goes in v7:
time: 68.4 us; the launch traced here: 68.3 us
  Pallas kernels  67.6 us (99%)
    pallas_call x1, Pallas kernels, run_step(): pl.pallas_call(step_kernel, out_shape=shapes, in_specs=[pl.BlockSpec(memo...  66.1 us
    pallas_call x1, Pallas kernels, run_step(): pl.pallas_call(emit_kernel, out_shape=shapes, in_specs=[any_spec] * 3, ou...  1.51 us

profile of v7, /device:TPU:0, one launch (start us, length us, event | category | flops | bytes accessed | tf_op | source)
XLA Modules:
  0.0 68.3 jit_solution(13336324633378469469)
XLA Ops:
  0.6 66.1 %decode_step.1 = (bf16[128,256]{1,0:T(8,128)(2,1)}, bf16[2,64,128]{2,1,0:T(8,128)(2,1)}, bf16[2,64,128]{2,1,0:T(8,128)(2,1)}) custom-call(bf16[128,256]{1,0:T(8,128)(2,1)} %refs_0_.1, s32[1,128]{1,0:T(1,128)} %bitcast.19, bf16[2,8192,512]{2,1,0:T(8,128)(2,1)} %bitcast.17, bf16[2,8192,512]{2,1,0:T(8,128)(2,1)} %bitcast.18, bf16[2,256]{1,0:T(2,128)(2,1)} %refs_4_.1, ...), custom_call_target="tpu_custom_call" | custom-call | tf_op jit(solution)/shard_map/decode_step/pallas_call | solution.py:533
  66.8 1.5 %emit.1 = (bf16[128,256]{1,0:T(8,128)(2,1)}, bf16[2,64,128]{2,1,0:T(8,128)(2,1)}, bf16[2,64,128]{2,1,0:T(8,128)(2,1)}) custom-call(bf16[128,256]{1,0:T(8,128)(2,1)} %get-tuple-element.9.h_in, bf16[2,64,128]{2,1,0:T(8,128)(2,1)} %get-tuple-element.10.k_in, bf16[2,64,128]{2,1,0:T(8,128)(2,1)} %get-tuple-element.11.v_in), custom_call_target="tpu_custom_call" | custom-call | tf_op jit(solution)/shard_map/emit/pallas_call | solution.py:543

commit v8 on v7

--- a/solution.py
+++ b/solution.py
@@ -18,7 +18,7 @@
 ROWS = BATCH // STREAMS
 HALF = ROWS // 2
 GROUP = 16
-COL_PIECES = 4
+COL_PIECES = 2
 N_ROW = 4
 N_COL = 4
 HEAD = 64
@@ -96,17 +96,15 @@
         load(("kv", layer, stream, which), src.at[layer, span], dst.at[layer, span],
              big_sem.at[(layer * STREAMS + stream) * 2 + which])
 
-    for stream in range(STREAMS):
-        for which in range(2):
-            big(0, stream, which)
-    for name, src, dst in (("wo", wo_in, wo), ("wf1", wf1_in, wf1), ("wf2", wf2_in, wf2)):
-        small((name, 0), src.at[0], dst.at[0])
-    for name, src, dst in (("wq", wq_in, wq), ("wk", wk_in, wk), ("wv", wv_in, wv), ("wo", wo_in, wo),
-                           ("wf1", wf1_in, wf1), ("wf2", wf2_in, wf2)):
-        small((name, 1), src.at[1], dst.at[1])
-    for stream in range(STREAMS):
-        for which in range(2):
-            big(1, stream, which)
+    def late_loads(layer):
+        for stream in range(STREAMS):
+            for which in range(2):
+                big(layer, stream, which)
+        names = (("wo", wo_in, wo), ("wf1", wf1_in, wf1), ("wf2", wf2_in, wf2))
+        if layer:
+            names += (("wq", wq_in, wq), ("wk", wk_in, wk), ("wv", wv_in, wv))
+        for name, src, dst in names:
+            small((name, layer), src.at[layer], dst.at[layer])
 
     waited = set()
 
@@ -130,7 +128,7 @@
         recvs[tag] = pltpu.make_async_copy(span, span, recv_sem.at[index])
 
     def to_col(tag, buf):
-        peers = (3 - col, lax.rem(col + 2, N_COL), col + 1 - 2 * lax.rem(col, 2))
+        peers = [lax.rem(col + off, N_COL) for off in (2, 3, 1)]
         rows = ROWS // COL_PIECES
         copies = []
         for piece in range(COL_PIECES):
@@ -432,6 +430,7 @@
     for stream in range(STREAMS):
         send_qkv(0, stream)
     send_affine(0, 0)
+    late_loads(0)
     need("len")
     len_mat[...] = jnp.transpose(jnp.broadcast_to(len_buf[...].astype(F32), (128, 128)))
     for layer in range(LAYERS):
@@ -445,14 +444,16 @@
         for stream in range(STREAMS):
             project(layer, stream)
         if layer == 0:
+            late_loads(1)
+        for stream in range(STREAMS):
+            send_inner(layer, stream)
+        for stream in range(STREAMS):
+            send_pair(layer, stream)
+        if layer == 0:
             for name in MAT_NAMES[:3]:
                 need((name, 1))
             send_affine(1, 0)
             send_affine(1, 1)
-        for stream in range(STREAMS):
-            send_inner(layer, stream)
-        for stream in range(STREAMS):
-            send_pair(layer, stream)
         for stream in range(STREAMS):
             send_act(layer, stream)
         for stream in range(STREAMS):

time: 68.4 us -> 69.8 us (1.020)
  Pallas kernels: 67.6 us -> 69 us
    pallas_call x1, Pallas kernels: 66.1 us -> 67.4 us  [run_step(): pl.pallas_call(step_kernel, out_shape=shapes, in_specs=[pl.BlockSpec(memo...]
where the time goes in v8:
time: 69.8 us; the launch traced here: 69.6 us
  Pallas kernels  69 us (99%)
    pallas_call x1, Pallas kernels, run_step(): pl.pallas_call(step_kernel, out_shape=shapes, in_specs=[pl.BlockSpec(memo...  67.4 us
    pallas_call x1, Pallas kernels, run_step(): pl.pallas_call(emit_kernel, out_shape=shapes, in_specs=[any_spec] * 3, ou...  1.51 us

profile of v8, /device:TPU:0, one launch (start us, length us, event | category | flops | bytes accessed | tf_op | source)
XLA Modules:
  0.0 69.6 jit_solution(12398401714732349558)
XLA Ops:
  0.6 67.4 %decode_step.1 = (bf16[128,256]{1,0:T(8,128)(2,1)}, bf16[2,64,128]{2,1,0:T(8,128)(2,1)}, bf16[2,64,128]{2,1,0:T(8,128)(2,1)}) custom-call(bf16[128,256]{1,0:T(8,128)(2,1)} %refs_0_.1, s32[1,128]{1,0:T(1,128)} %bitcast.19, bf16[2,8192,512]{2,1,0:T(8,128)(2,1)} %bitcast.17, bf16[2,8192,512]{2,1,0:T(8,128)(2,1)} %bitcast.18, bf16[2,256]{1,0:T(2,128)(2,1)} %refs_4_.1, ...), custom_call_target="tpu_custom_call" | custom-call | tf_op jit(solution)/shard_map/decode_step/pallas_call | solution.py:534
  68.1 1.5 %emit.1 = (bf16[128,256]{1,0:T(8,128)(2,1)}, bf16[2,64,128]{2,1,0:T(8,128)(2,1)}, bf16[2,64,128]{2,1,0:T(8,128)(2,1)}) custom-call(bf16[128,256]{1,0:T(8,128)(2,1)} %get-tuple-element.9.h_in, bf16[2,64,128]{2,1,0:T(8,128)(2,1)} %get-tuple-element.10.k_in, bf16[2,64,128]{2,1,0:T(8,128)(2,1)} %get-tuple-element.11.v_in), custom_call_target="tpu_custom_call" | custom-call | tf_op jit(solution)/shard_map/emit/pallas_call | solution.py:544

commit v9 on v7

--- a/solution.py
+++ b/solution.py
@@ -80,10 +80,14 @@
         for name, src, dst in (("wq", wq_in, wq), ("wk", wk_in, wk), ("wv", wv_in, wv)):
             if layer == 0:
                 small((name, layer), src.at[layer], dst.at[layer])
+    for name, src, dst in (("wq", wq_in, wq), ("wk", wk_in, wk), ("wv", wv_in, wv)):
+        small((name, 1), src.at[1], dst.at[1])
     for name, src, dst in (("b1", b1_in, b1), ("bq", bq_in, bq), ("bk", bk_in, bk), ("bv", bv_in, bv),
                            ("len", len_in, len_buf), ("bo", bo_in, bo), ("g2", g2_in, g2), ("b2", b2_in, b2),
                            ("bf1", bf1_in, bf1), ("bf2", bf2_in, bf2)):
         small(name, src, dst)
+    for layer in range(LAYERS):
+        small(("wf1", layer), wf1_in.at[layer], wf1.at[layer])
 
     barrier = pltpu.get_barrier_semaphore()
     for off in range(1, 4):
@@ -99,10 +103,9 @@
     for stream in range(STREAMS):
         for which in range(2):
             big(0, stream, which)
-    for name, src, dst in (("wo", wo_in, wo), ("wf1", wf1_in, wf1), ("wf2", wf2_in, wf2)):
+    for name, src, dst in (("wo", wo_in, wo), ("wf2", wf2_in, wf2)):
         small((name, 0), src.at[0], dst.at[0])
-    for name, src, dst in (("wq", wq_in, wq), ("wk", wk_in, wk), ("wv", wv_in, wv), ("wo", wo_in, wo),
-                           ("wf1", wf1_in, wf1), ("wf2", wf2_in, wf2)):
+    for name, src, dst in (("wo", wo_in, wo), ("wf2", wf2_in, wf2)):
         small((name, 1), src.at[1], dst.at[1])
     for stream in range(STREAMS):
         for which in range(2):
@@ -214,66 +217,68 @@
         to_axis(("st1", slot), "row", lambda d: st_send.at[2 * slot], st_recv.at[2 * slot])
         to_axis(("qkv", slot), "row", lambda d: qkv_send.at[slot, d], qkv_recv.at[slot])
 
-    def affine_rows(gain, shift):
+    def affine_rows(gains, shifts, layer):
+        gain, shift = gains[layer:layer + 1, :].astype(F32), shifts[layer:layer + 1, :].astype(F32)
         sub = lax.broadcasted_iota(jnp.int32, (16, WIDTH), 0)
-        return jnp.where(sub == 0, gain.astype(F32), jnp.where(sub == 1, shift.astype(F32), 0.0)).astype(BF16)
-
-    def send_affine(layer, kind):
+        return jnp.where(sub == 2 * layer, gain, jnp.where(sub == 2 * layer + 1, shift, 0.0)).astype(BF16)
+
+    def send_affine(kind):
         bias_on = jnp.where(row == 0, 1.0, 0.0)
+
+        def product(gains, shifts, w, b):
+            total = None
+            for layer in range(LAYERS):
+                part = dot(affine_rows(gains, shifts, layer), w[layer])[0:8]
+                sub = lax.broadcasted_iota(jnp.int32, part.shape, 0)
+                part = part + jnp.where(sub == 2 * layer + 1, b[layer:layer + 1, :].astype(F32) * bias_on, 0.0)
+                total = part if total is None else total + part
+            return total
+
         if kind == 0:
-            for name in ("b1", "bq", "bk", "bv"):
+            for name in ("b1", "bq", "bk", "bv", ("wq", 1), ("wk", 1), ("wv", 1)):
                 need(name)
-            rows = affine_rows(g1[layer:layer + 1, :], b1[layer:layer + 1, :])
-            parts = []
-            for w, b in ((wq, bq), (wk, bk), (wv, bv)):
-                bias = b[layer:layer + 1, :].astype(F32) * bias_on
-                part = dot(rows, w[layer])[0:8]
-                sub_w = lax.broadcasted_iota(jnp.int32, (8, WIDTH), 0)
-                parts.append(part + jnp.where(sub_w == 1, bias, 0.0))
-            q, k, v = parts
+            q, k, v = product(g1, b1, wq, bq), product(g1, b1, wk, bk), product(g1, b1, wv, bv)
             for j in range(N_ROW):
                 lo = (j // 2) * 128
                 qj, kj, vj = q[:, lo:lo + 128], k[:, lo:lo + 128], v[:, lo:lo + 128]
                 if j % 2 == 0:
                     first = jnp.where(low_half((8, 128)), qj, swap_halves(kj))
-                    second = jnp.where(low_half((8, 128)), vj, swap_halves(vj))
                 else:
                     first = jnp.where(low_half((8, 128)), swap_halves(qj), kj)
-                    second = jnp.where(low_half((8, 128)), swap_halves(vj), vj)
-                gq_send[layer, j] = jnp.concatenate([first, second], axis=1)
-            gq_recv[layer, row] = gq_send[layer, row]
-            to_axis(("gb", layer, kind), "row", lambda d: gq_send.at[layer, d], gq_recv.at[layer])
+                    vj = swap_halves(vj)
+                second = jnp.where(low_half((8, 128)), vj, swap_halves(vj))
+                gq_send[j] = jnp.concatenate([first, second], axis=1)
+            gq_recv[row] = gq_send[row]
+            to_axis(("gb", kind), "row", lambda d: gq_send.at[d], gq_recv)
         else:
-            for name in ("g2", "b2", "bf1", ("wf1", layer)):
+            for name in ("g2", "b2", "bf1", ("wf1", 0), ("wf1", 1)):
                 need(name)
-            rows = affine_rows(g2[layer:layer + 1, :], b2[layer:layer + 1, :])
-            part = dot(rows, wf1[layer])[0:8]
-            sub_w = lax.broadcasted_iota(jnp.int32, (8, FF_LOC), 0)
-            part = part + jnp.where(sub_w == 1, bf1[layer:layer + 1, :].astype(F32) * bias_on, 0.0)
+            part = product(g2, b2, wf1, bf1)
             for j in range(2):
-                gf_send[layer, j] = part[:, j * FF_HALF:(j + 1) * FF_HALF]
-            gf_recv[layer, row] = gf_send[layer, side]
-            to_axis(("gb", layer, kind), "row", lambda d: gf_send.at[layer, lax.rem(d, 2)], gf_recv.at[layer])
+                gf_send[j] = part[:, j * FF_HALF:(j + 1) * FF_HALF]
+            gf_recv[row] = gf_send[side]
+            to_axis(("gb", kind), "row", lambda d: gf_send.at[lax.rem(d, 2)], gf_recv)
 
     gb_done = set()
 
-    def affine_lines(layer, kind):
-        if (layer, kind) not in gb_done:
-            gb_done.add((layer, kind))
-            arrived(("gb", layer, kind))
+    def affine_lines(kind):
+        if kind not in gb_done:
+            gb_done.add(kind)
+            arrived(("gb", kind))
 
     def gain_line(buf, layer, r):
-        return buf[layer, r, 0:1]
+        return buf[r, 2 * layer:2 * layer + 1]
 
     def const_line(buf, layer):
-        return buf[layer, 0, 1:2] + buf[layer, 1, 1:2] + buf[layer, 2, 1:2] + buf[layer, 3, 1:2]
+        at = slice(2 * layer + 1, 2 * layer + 2)
+        return buf[0, at] + buf[1, at] + buf[2, at] + buf[3, at]
 
     def attend(layer, stream):
         slot = layer * STREAMS + stream
         span = slice(stream * ROWS, (stream + 1) * ROWS)
         arrived(("st1", slot))
         cols = stat_columns([block_stats(2 * slot, r) for r in range(N_ROW)])
-        affine_lines(layer, 0)
+        affine_lines(0)
         gains = [gain_line(gq_recv, layer, r) for r in range(N_ROW)]
         const = const_line(gq_recv, layer)
         arrived(("qkv", slot))
@@ -386,7 +391,7 @@
         slot = layer * STREAMS + stream
         arrived(("st2", slot))
         cols = stat_columns([block_stats(2 * slot + 1, r) for r in (row, partner)])
-        affine_lines(layer, 1)
+        affine_lines(1)
         arrived(("f1", slot))
         total = f1_mine[stream] * cols[0] + cols[2] * gain_line(gf_recv, layer, row)
         total = total + f1_recv[slot].astype(F32) * cols[1] + cols[3] * gain_line(gf_recv, layer, partner)
@@ -431,7 +436,8 @@
 
     for stream in range(STREAMS):
         send_qkv(0, stream)
-    send_affine(0, 0)
+    send_affine(0)
+    send_affine(1)
     need("len")
     len_mat[...] = jnp.transpose(jnp.broadcast_to(len_buf[...].astype(F32), (128, 128)))
     for layer in range(LAYERS):
@@ -440,15 +446,8 @@
         kv_turn[layer] = jnp.transpose(kv_mix[layer]).astype(BF16)
         store(kv_turn.at[layer, 0:HEAD], k_out.at[layer], 2 * layer)
         store(kv_turn.at[layer, HEAD:2 * HEAD], v_out.at[layer], 2 * layer + 1)
-        if layer == 0:
-            send_affine(0, 1)
         for stream in range(STREAMS):
             project(layer, stream)
-        if layer == 0:
-            for name in MAT_NAMES[:3]:
-                need((name, 1))
-            send_affine(1, 0)
-            send_affine(1, 1)
         for stream in range(STREAMS):
             send_inner(layer, stream)
         for stream in range(STREAMS):
@@ -471,7 +470,7 @@
 
 
 N_SLOT = LAYERS * STREAMS
-N_COPY = 10 * N_SLOT + 2 * LAYERS
+N_COPY = 10 * N_SLOT + 2
 N_PEER = N_ROW + N_COL - 2
 
 
@@ -507,10 +506,10 @@
         vm((ROWS, 128), F32),
         vm((2 * N_SLOT, 8, 128), F32),
         vm((2 * N_SLOT, N_ROW, 8, 128), F32),
-        vm((LAYERS, N_ROW, 8, WIDTH), F32),
-        vm((LAYERS, N_ROW, 8, WIDTH), F32),
-        vm((LAYERS, 2, 8, FF_HALF), F32),
-        vm((LAYERS, N_ROW, 8, FF_HALF), F32),
+        vm((N_ROW, 8, WIDTH), F32),
+        vm((N_ROW, 8, WIDTH), F32),
+        vm((2, 8, FF_HALF), F32),
+        vm((N_ROW, 8, FF_HALF), F32),
         vm((N_SLOT, N_ROW, ROWS + HALF, 128), BF16),
         vm((N_SLOT, N_ROW, ROWS + HALF, 128), BF16),
         vm((N_SLOT, N_ROW, HALF, 128), BF16),

time: 68.4 us -> 68.5 us (level)
  no operation moved by 1% of the time
where the time goes in v9:
time: 68.5 us; the launch traced here: 68.3 us
  Pallas kernels  67.6 us (99%)
    pallas_call x1, Pallas kernels, run_step(): pl.pallas_call(step_kernel, out_shape=shapes, in_specs=[pl.BlockSpec(memo...  66.1 us
    pallas_call x1, Pallas kernels, run_step(): pl.pallas_call(emit_kernel, out_shape=shapes, in_specs=[any_spec] * 3, ou...  1.51 us

profile of v9, /device:TPU:0, one launch (start us, length us, event | category | flops | bytes accessed | tf_op | source)
XLA Modules:
  0.0 68.3 jit_solution(8874119699468301172)
XLA Ops:
  0.6 66.1 %decode_step.1 = (bf16[128,256]{1,0:T(8,128)(2,1)}, bf16[2,64,128]{2,1,0:T(8,128)(2,1)}, bf16[2,64,128]{2,1,0:T(8,128)(2,1)}) custom-call(bf16[128,256]{1,0:T(8,128)(2,1)} %refs_0_.1, s32[1,128]{1,0:T(1,128)} %bitcast.19, bf16[2,8192,512]{2,1,0:T(8,128)(2,1)} %bitcast.17, bf16[2,8192,512]{2,1,0:T(8,128)(2,1)} %bitcast.18, bf16[2,256]{1,0:T(2,128)(2,1)} %refs_4_.1, ...), custom_call_target="tpu_custom_call" | custom-call | tf_op jit(solution)/shard_map/decode_step/pallas_call | solution.py:532
  66.8 1.5 %emit.1 = (bf16[128,256]{1,0:T(8,128)(2,1)}, bf16[2,64,128]{2,1,0:T(8,128)(2,1)}, bf16[2,64,128]{2,1,0:T(8,128)(2,1)}) custom-call(bf16[128,256]{1,0:T(8,128)(2,1)} %get-tuple-element.9.h_in, bf16[2,64,128]{2,1,0:T(8,128)(2,1)} %get-tuple-element.10.k_in, bf16[2,64,128]{2,1,0:T(8,128)(2,1)} %get-tuple-element.11.v_in), custom_call_target="tpu_custom_call" | custom-call | tf_op jit(solution)/shard_map/emit/pallas_call | solution.py:542

commit v10 on v9

--- a/solution.py
+++ b/solution.py
@@ -49,10 +49,10 @@
      wo_in, bo_in, g2_in, b2_in, wf1_in, bf1_in, wf2_in, bf2_in,
      h_out, k_out, v_out,
      x_buf, len_buf, k_buf, v_buf, g1, b1, wq, bq, wk, bk, wv, bv, wo, bo, g2, b2, wf1, bf1, wf2, bf2,
-     len_mat, kv_mix, kv_turn, s_buf, p_buf, o_mix,
+     len_mat, kv_mix, s_buf, p_buf, o_mix,
      st_send, st_recv, gq_send, gq_recv, gf_send, gf_recv, qkv_send, qkv_recv, o_recv,
      proj_recv, f1_mine, f1_send, f1_recv, pair_recv, u_recv, out_recv,
-     load_sem, big_sem, store_sem, send_sem, recv_sem) = refs
+     load_sem, big_sem, send_sem, recv_sem) = refs
 
     row = lax.axis_index("row")
     col = lax.axis_index("col")
@@ -427,13 +427,6 @@
         arrived(("out", slot))
         residual(col_sum(out_recv.at[slot]), bf2[layer:layer + 1, :].astype(F32), stream)
 
-    stores = []
-
-    def store(src, dst, index):
-        copy = pltpu.make_async_copy(src, dst, store_sem.at[index])
-        copy.start()
-        stores.append(copy)
-
     for stream in range(STREAMS):
         send_qkv(0, stream)
     send_affine(0)
@@ -443,9 +436,9 @@
     for layer in range(LAYERS):
         for stream in range(STREAMS):
             attend(layer, stream)
-        kv_turn[layer] = jnp.transpose(kv_mix[layer]).astype(BF16)
-        store(kv_turn.at[layer, 0:HEAD], k_out.at[layer], 2 * layer)
-        store(kv_turn.at[layer, HEAD:2 * HEAD], v_out.at[layer], 2 * layer + 1)
+        turned = jnp.transpose(kv_mix[layer]).astype(BF16)
+        k_out[layer] = turned[0:HEAD]
+        v_out[layer] = turned[HEAD:2 * HEAD]
         for stream in range(STREAMS):
             project(layer, stream)
         for stream in range(STREAMS):
@@ -461,10 +454,8 @@
             if layer + 1 < LAYERS:
                 send_qkv(layer + 1, stream)
             else:
-                span = pl.ds(stream * ROWS, ROWS)
-                store(x_buf.at[span], h_out.at[span], 2 * LAYERS + stream)
-    for copy in stores:
-        copy.wait()
+                span = slice(stream * ROWS, (stream + 1) * ROWS)
+                h_out[span, :] = x_buf[span, :]
     for copy in drains:
         copy.wait()
 
@@ -474,18 +465,12 @@
 N_PEER = N_ROW + N_COL - 2
 
 
-def emit_kernel(h_in, k_in, v_in, h_out, k_out, v_out, h_buf, k_buf, v_buf, sem):
-    moves = ((h_in, h_buf, h_out), (k_in, k_buf, k_out), (v_in, v_buf, v_out))
-    loads = [pltpu.make_async_copy(src, buf, sem.at[i]) for i, (src, buf, _) in enumerate(moves)]
-    for copy in loads:
+def emit_kernel(h_in, k_in, v_in, h_out, k_out, v_out, sem):
+    copies = [pltpu.make_async_copy(src, dst, sem.at[i])
+              for i, (src, dst) in enumerate(((h_in, h_out), (k_in, k_out), (v_in, v_out)))]
+    for copy in copies:
         copy.start()
-    stores = []
-    for i, (_, buf, dst) in enumerate(moves):
-        loads[i].wait()
-        copy = pltpu.make_async_copy(buf, dst, sem.at[i])
-        copy.start()
-        stores.append(copy)
-    for copy in stores:
+    for copy in copies:
         copy.wait()
 
 
@@ -500,7 +485,6 @@
     scratch = in_scratch + [
         vm((BATCH, 128), F32),
         vm((LAYERS, BATCH, 128), F32),
-        vm((LAYERS, BATCH, 128), BF16),
         vm((ROWS, SEQ), F32),
         vm((ROWS, SEQ), BF16),
         vm((ROWS, 128), F32),
@@ -522,18 +506,18 @@
         vm((N_SLOT, N_COL, ROWS, WIDTH), BF16),
         pltpu.SemaphoreType.DMA((32,)),
         pltpu.SemaphoreType.DMA((2 * N_SLOT,)),
-        pltpu.SemaphoreType.DMA((2 * LAYERS + STREAMS,)),
         pltpu.SemaphoreType.DMA((N_COPY,)),
         pltpu.SemaphoreType.DMA((N_COPY,)),
     ]
     shapes = (jax.ShapeDtypeStruct((BATCH, WIDTH), BF16),
               jax.ShapeDtypeStruct((LAYERS, HEAD, BATCH), BF16),
               jax.ShapeDtypeStruct((LAYERS, HEAD, BATCH), BF16))
+    vmem_spec = pl.BlockSpec(memory_space=pltpu.VMEM)
     results = pl.pallas_call(
         step_kernel,
-        out_shape=shapes,
+        out_shape=tuple(vm(a.shape, a.dtype) for a in shapes),
         in_specs=[pl.BlockSpec(memory_space=pltpu.HBM)] * len(args),
-        out_specs=(any_spec,) * 3,
+        out_specs=(vmem_spec,) * 3,
         scratch_shapes=scratch,
         compiler_params=pltpu.CompilerParams(
             collective_id=0, has_side_effects=True, vmem_limit_bytes=60 * 1024 * 1024),
@@ -542,10 +526,10 @@
     h_out, k_new, v_new = pl.pallas_call(
         emit_kernel,
         out_shape=shapes,
-        in_specs=[any_spec] * 3,
-        out_specs=(pl.BlockSpec(memory_space=pltpu.HBM),) * 3,
-        scratch_shapes=[vm(a.shape, a.dtype) for a in shapes] + [pltpu.SemaphoreType.DMA((3,))],
-        compiler_params=pltpu.CompilerParams(vmem_limit_bytes=60 * 1024 * 1024),
+        in_specs=[vmem_spec] * 3,
+        out_specs=(any_spec,) * 3,
+        scratch_shapes=[pltpu.SemaphoreType.DMA((3,))],
+        compiler_params=pltpu.CompilerParams(vmem_limit_bytes=1024 * 1024),
         name="emit",
     )(*results)
 

time: 68.5 us -> 67.1 us (0.980)
  Pallas kernels: 67.6 us -> 66.3 us
    pallas_call x2, Pallas kernels: 67.6 us -> 66.3 us  [the longest x1 65.6 us: run_step(): pl.pallas_call(step_kernel, out_shape=tuple((vm(a.shape, a.dtype) for a i...]
where the time goes in v10:
time: 67.1 us; the launch traced here: 66.9 us
  Pallas kernels  66.3 us (99%)
    pallas_call x1, Pallas kernels, run_step(): pl.pallas_call(step_kernel, out_shape=tuple((vm(a.shape, a.dtype) for a i...  65.6 us

profile of v10, /device:TPU:0, one launch (start us, length us, event | category | flops | bytes accessed | tf_op | source)
XLA Modules:
  0.0 66.9 jit_solution(16724794254850425053)
XLA Ops:
  0.6 65.6 %decode_step.1 = (bf16[128,256]{1,0:T(8,128)(2,1)S(1)}, bf16[2,64,128]{2,1,0:T(8,128)(2,1)S(1)}, bf16[2,64,128]{2,1,0:T(8,128)(2,1)S(1)}) custom-call(bf16[128,256]{1,0:T(8,128)(2,1)} %refs_0_.1, s32[1,128]{1,0:T(1,128)} %bitcast.19, bf16[2,8192,512]{2,1,0:T(8,128)(2,1)} %bitcast.17, bf16[2,8192,512]{2,1,0:T(8,128)(2,1)} %bitcast.18, ...), custom_call_target="tpu_custom_call" | custom-call | tf_op jit(solution)/shard_map/decode_step/pallas_call | solution.py:516
  66.3 0.7 %emit.1 = (bf16[128,256]{1,0:T(8,128)(2,1)}, bf16[2,64,128]{2,1,0:T(8,128)(2,1)}, bf16[2,64,128]{2,1,0:T(8,128)(2,1)}) custom-call(bf16[128,256]{1,0:T(8,128)(2,1)S(1)} %get-tuple-element.9.h_in, bf16[2,64,128]{2,1,0:T(8,128)(2,1)S(1)} %get-tuple-element.10.k_in, bf16[2,64,128]{2,1,0:T(8,128)(2,1)S(1)} %get-tuple-element.11.v_in), custom_call_target="tpu_custom_call" | custom-call | tf_op jit(solution)/shard_map/emit/pallas_call | solution.py:526

commit v11 on v10

--- a/solution.py
+++ b/solution.py
@@ -18,7 +18,7 @@
 ROWS = BATCH // STREAMS
 HALF = ROWS // 2
 GROUP = 16
-COL_PIECES = 4
+COL_PIECES = 2
 N_ROW = 4
 N_COL = 4
 HEAD = 64
@@ -133,7 +133,7 @@
         recvs[tag] = pltpu.make_async_copy(span, span, recv_sem.at[index])
 
     def to_col(tag, buf):
-        peers = (3 - col, lax.rem(col + 2, N_COL), col + 1 - 2 * lax.rem(col, 2))
+        peers = [lax.rem(col + off, N_COL) for off in (2, 3, 1)]
         rows = ROWS // COL_PIECES
         copies = []
         for piece in range(COL_PIECES):

time: 67.1 us -> 68.1 us (1.015)
  Pallas kernels: 66.3 us -> 67.3 us
    pallas_call x1, Pallas kernels: 65.6 us -> 66.6 us  [run_step(): pl.pallas_call(step_kernel, out_shape=tuple((vm(a.shape, a.dtype) for a i...]
where the time goes in v11:
time: 68.1 us; the launch traced here: 67.9 us
  Pallas kernels  67.3 us (99%)
    pallas_call x1, Pallas kernels, run_step(): pl.pallas_call(step_kernel, out_shape=tuple((vm(a.shape, a.dtype) for a i...  66.6 us

profile of v11, /device:TPU:0, one launch (start us, length us, event | category | flops | bytes accessed | tf_op | source)
XLA Modules:
  0.0 67.9 jit_solution(2605966702318614955)
XLA Ops:
  0.6 66.6 %decode_step.1 = (bf16[128,256]{1,0:T(8,128)(2,1)S(1)}, bf16[2,64,128]{2,1,0:T(8,128)(2,1)S(1)}, bf16[2,64,128]{2,1,0:T(8,128)(2,1)S(1)}) custom-call(bf16[128,256]{1,0:T(8,128)(2,1)} %refs_0_.1, s32[1,128]{1,0:T(1,128)} %bitcast.19, bf16[2,8192,512]{2,1,0:T(8,128)(2,1)} %bitcast.17, bf16[2,8192,512]{2,1,0:T(8,128)(2,1)} %bitcast.18, ...), custom_call_target="tpu_custom_call" | custom-call | tf_op jit(solution)/shard_map/decode_step/pallas_call | solution.py:516
  67.3 0.7 emit.1

commit v12 on v10

--- a/solution.py
+++ b/solution.py
@@ -18,7 +18,7 @@
 ROWS = BATCH // STREAMS
 HALF = ROWS // 2
 GROUP = 16
-COL_PIECES = 4
+COL_PIECES = 1
 N_ROW = 4
 N_COL = 4
 HEAD = 64

time: 67.1 us -> 67 us (level)
  no operation moved by 1% of the time
where the time goes in v12:
time: 67 us; the launch traced here: 66.9 us
  Pallas kernels  66.2 us (99%)
    pallas_call x1, Pallas kernels, run_step(): pl.pallas_call(step_kernel, out_shape=tuple((vm(a.shape, a.dtype) for a i...  65.5 us

profile of v12, /device:TPU:0, one launch (start us, length us, event | category | flops | bytes accessed | tf_op | source)
XLA Modules:
  0.0 66.9 jit_solution(10450166039844804004)
XLA Ops:
  0.6 65.5 %decode_step.1 = (bf16[128,256]{1,0:T(8,128)(2,1)S(1)}, bf16[2,64,128]{2,1,0:T(8,128)(2,1)S(1)}, bf16[2,64,128]{2,1,0:T(8,128)(2,1)S(1)}) custom-call(bf16[128,256]{1,0:T(8,128)(2,1)} %refs_0_.1, s32[1,128]{1,0:T(1,128)} %bitcast.19, bf16[2,8192,512]{2,1,0:T(8,128)(2,1)} %bitcast.17, bf16[2,8192,512]{2,1,0:T(8,128)(2,1)} %bitcast.18, ...), custom_call_target="tpu_custom_call" | custom-call | tf_op jit(solution)/shard_map/decode_step/pallas_call | solution.py:516
  66.2 0.7 %emit.1 = (bf16[128,256]{1,0:T(8,128)(2,1)}, bf16[2,64,128]{2,1,0:T(8,128)(2,1)}, bf16[2,64,128]{2,1,0:T(8,128)(2,1)}) custom-call(bf16[128,256]{1,0:T(8,128)(2,1)S(1)} %get-tuple-element.9.h_in, bf16[2,64,128]{2,1,0:T(8,128)(2,1)S(1)} %get-tuple-element.10.k_in, bf16[2,64,128]{2,1,0:T(8,128)(2,1)S(1)} %get-tuple-element.11.v_in), custom_call_target="tpu_custom_call" | custom-call | tf_op jit(solution)/shard_map/emit/pallas_call | solution.py:526
